TPU v7x, 512 devices: a whole 4x8x8 slice. The times are simulated.
512 devices in a mesh: freq: 128 (over y, z, core), rows: 4 (over x).
Axes of the slice: x: 4, y: 8, z: 8, core: 2. Of those that a mesh axis runs over, the one named last changes fastest.
Arguments:
- wavefield: bfloat16 [10240, 32, 1024], P('freq', 'rows'), may hold values from -6 to 6
- u_factors: bfloat16 [2, 256, 4, 256, 512], P(None, 'freq', 'rows'), may hold values from -0.25 to 0.25
- v_factors: bfloat16 [2, 256, 4, 512, 256], P(None, 'freq', 'rows'), may hold values from -0.375 to 0.375
- tile_ranks: int32 [256, 4, 40], P('freq', 'rows'), may hold values from 1 to 64, as said below
- tile_offsets: int32 [256, 4, 40], P('freq', 'rows'), may hold values from 0 to 511, as said below
Outputs:
- convolved: bfloat16 [1024, 32, 1024], P(('rows', 'freq'))
Inputs may be any that keep to these rules, and one draw needn't show every extreme that they name: tile_ranks[k, i, j] is the rank of tile (i, j) of frequency k; the ranks of one tile row sum to at most 512, exactly 512 on some row of every draw, and every tile row has a tile of rank 64. tile_offsets[k, i, j] is the sum of tile_ranks[k, i, j2] over j2 < j.
All inputs are finite; a program needn't handle non-finite values.
Results may differ from a plain program's by a relative error of at most 0.0072.
Values may be sent and summed in bfloat16 or wider, within the bound.
A program may use at most 128 MiB of HBM per device.

v0:
```python
import functools
import math

import jax
import jax.numpy as jnp
from jax import lax
from jax.sharding import Mesh
from jax.sharding import PartitionSpec as P

RANK_MAX = 64
FREQ = ("freq_0", "freq_1", "freq_2")
ROWS_FREQ = ("rows", "freq_0", "freq_1", "freq_2")


def from_everyone(value, axis):
    copies = jnp.broadcast_to(value, (lax.axis_size(axis), *value.shape))
    return lax.all_to_all(copies, axis, split_axis=0, concat_axis=0, tiled=True)


def joined_along(parts, dim):
    parts = jnp.moveaxis(parts, 0, dim)
    dims = parts.shape
    return parts.reshape(*dims[:dim], dims[dim] * dims[dim + 1], *dims[dim + 2 :])


def gathered_copies(value, axis, dim):
    parts = from_everyone(value, axis)
    return joined_along(parts, dim)


def cut_along(value, dim, devices):
    before, after = (value.shape[:dim], value.shape[dim + 1 :])
    return jnp.moveaxis(value.reshape(*before, devices, -1, *after), dim, 0)


def turned_blocks(parts, axes, turns):
    dims = [lax.axis_size(a) for a in axes]
    parts = parts.reshape(*dims, *parts.shape[1:])
    for k in turns:
        parts = lax.all_to_all(parts, axes[k], split_axis=k, concat_axis=k, tiled=True)
    return parts.reshape(-1, *parts.shape[len(axes) :])


def two_step_exchange(value, groups, turns, split_dim, concat_dim):
    devices = lax.axis_size(groups[0]) * lax.axis_size(groups[1])
    parts = cut_along(value, split_dim, devices)
    return joined_along(turned_blocks(parts, groups, turns), concat_dim)


def spectral_tables(freq_count, sample_count):
    freq_bins = jnp.arange(freq_count, dtype=jnp.int32) + 1
    sample_index = jnp.arange(sample_count, dtype=jnp.int32)
    phase_int = freq_bins[:, None] * sample_index[None, :] % sample_count
    angles = phase_int.astype(jnp.float32) * (2.0 * math.pi / sample_count)
    cosine = jnp.cos(angles)
    minus_sine = -jnp.sin(angles)
    stacked = jnp.stack([cosine, minus_sine], axis=1)
    forward = (stacked / math.sqrt(sample_count)).astype(jnp.bfloat16)
    inverse = (stacked / math.sqrt(freq_count)).astype(jnp.bfloat16)
    return (forward, inverse)


def tile_windows(v_row, u_row, starts, rank_max):
    columns = starts.shape[0]
    slot_index = (starts[:, None] + jnp.arange(rank_max, dtype=jnp.int32)[None, :]).reshape(-1)
    v_padded = jnp.pad(v_row, ((0, 0), (0, rank_max), (0, 0)))
    u_padded = jnp.pad(u_row, ((0, 0), (0, 0), (0, rank_max)))
    v_win = jnp.take(v_padded, slot_index, axis=1).reshape(2, columns, rank_max, v_row.shape[2])
    u_win = jnp.take(u_padded, slot_index, axis=2).reshape(2, u_row.shape[1], columns, rank_max)
    return (v_win, u_win)


def slot_lookup(starts, counts, rank_max, slot_count):
    position = jnp.arange(slot_count, dtype=jnp.int32)
    started = starts[:, None, :] <= position[None, :, None]
    owner_tile = jnp.sum(started.astype(jnp.int32), axis=2) - 1
    first_slot = jnp.max(jnp.where(started, starts[:, None, :], 0), axis=2)
    within = position[None, :] - first_slot
    live_slot = position[None, :] < (starts[:, -1] + counts[:, -1])[:, None]
    flat_index = jnp.where(live_slot, owner_tile * rank_max + within, 0)
    return (flat_index, live_slot)


def take_slots(values, chosen):
    return jnp.take(values, chosen, axis=1)


def per_device(wavefield, u_factors, v_factors, tile_ranks, tile_offsets):
    rec_dev, src_dev, samples = wavefield.shape
    freq_dev = u_factors.shape[1]
    rows_dev = u_factors.shape[2]
    tile_size = u_factors.shape[3]
    slot_count = u_factors.shape[4]
    freq_group = lax.axis_size(FREQ)
    row_group = lax.axis_size("rows")
    freqs = freq_dev * freq_group
    receivers = rec_dev * freq_group
    columns = receivers // tile_size
    sources = src_dev * row_group
    forward, inverse = spectral_tables(freqs, samples)
    spectrum = jnp.einsum("kct,rst->kcrs", forward, wavefield, preferred_element_type=jnp.float32)
    spectrum = spectrum.astype(jnp.bfloat16).reshape(freqs, 2, rec_dev * src_dev)
    windows = jax.vmap(
        functools.partial(tile_windows, rank_max=RANK_MAX), in_axes=(1, 1, 0), out_axes=(1, 1)
    )
    rank_slots = jnp.arange(RANK_MAX, dtype=jnp.int32)
    tile_row = 0
    v_win, u_win = windows(
        v_factors[:, :, tile_row], u_factors[:, :, tile_row], tile_offsets[:, tile_row]
    )
    rank_mask = rank_slots[None, None, :] < tile_ranks[:, tile_row, :, None]
    flat_index, live_slot = slot_lookup(
        tile_offsets[:, tile_row], tile_ranks[:, tile_row], RANK_MAX, slot_count
    )
    prepared = [(v_win, u_win, rank_mask, flat_index, live_slot)]
    by_frequency = lax.all_to_all(spectrum, FREQ, split_axis=0, concat_axis=2, tiled=True)
    portion = gathered_copies(by_frequency[None], "rows", 0)
    blocks_in = portion.shape[0]
    spectra = portion.reshape(blocks_in, freq_dev, 2, columns, tile_size, src_dev)
    spectra = jnp.transpose(spectra, (1, 2, 3, 4, 0, 5)).reshape(
        freq_dev, 2, columns, tile_size, blocks_in * src_dev
    )
    tile_row = 0
    v_win, u_win, rank_mask, flat_index, live_slot = prepared[tile_row]
    quadrants = jnp.einsum(
        "afjmr,fbjrs->fabjms", v_win, spectra, preferred_element_type=jnp.float32
    )
    coeffs = jnp.stack(
        [quadrants[:, 0, 0] - quadrants[:, 1, 1], quadrants[:, 0, 1] + quadrants[:, 1, 0]], axis=1
    )
    coeffs = jnp.where(rank_mask[:, None, :, :, None], coeffs, 0.0).astype(jnp.bfloat16)
    stacked = coeffs.reshape(freq_dev, 2, columns * RANK_MAX, blocks_in * src_dev)
    packed = jax.vmap(take_slots)(stacked, flat_index)
    packed = jnp.where(live_slot[:, None, :, None], packed, jnp.zeros((), jnp.bfloat16))
    products = jnp.einsum(
        "afrk,fcks->facrs", u_factors[:, :, tile_row], packed, preferred_element_type=jnp.float32
    )
    results = [
        jnp.stack(
            [products[:, 0, 0] - products[:, 1, 1], products[:, 0, 1] + products[:, 1, 0]], axis=1
        )
    ]
    merged = jnp.stack(results, axis=2)
    bands = merged.astype(jnp.bfloat16).reshape(
        freq_dev, 2, rows_dev * tile_size, blocks_in, src_dev
    )
    bands = bands.reshape(freq_dev, 2, rows_dev * tile_size * sources)
    returned = two_step_exchange(bands, (("freq_0", "freq_1"), "freq_2"), (1, 0), 2, 0)
    series = jnp.einsum("kcq,kct->qt", returned, inverse, preferred_element_type=jnp.float32)
    return series.astype(jnp.bfloat16).reshape(rows_dev * tile_size // freq_group, sources, samples)


def solution(mesh):
    torus = Mesh(
        mesh.devices.reshape(8, 8, 2, mesh.shape["rows"]), ("freq_0", "freq_1", "freq_2", "rows")
    )
    return jax.shard_map(
        per_device,
        mesh=torus,
        in_specs=(
            P(FREQ, "rows", None),
            P(None, FREQ, "rows", None, None),
            P(None, FREQ, "rows", None, None),
            P(FREQ, "rows", None),
            P(FREQ, "rows", None),
        ),
        out_specs=P(ROWS_FREQ, None, None),
        check_vma=False,
    )
```

profile of v0, /device:TPU:1, one launch (start us, length us, event | category | flops | bytes accessed | tf_op | source)
XLA Modules:
  0.0 269.1 jit_solution(7426933397756940463)
XLA Ops:
  0.0 4.2 %fusion.22 = (f32[256,1,1024]{2,0,1:T(8,128)S(1)}, f32[256,1,1024]{2,0,1:T(8,128)S(1)}) fusion(s32[256]{0:T(256)S(1)} %iota_add_fusion), kind=kLoop, calls=%fused_computation.36 | loop fusion | flops 3932160 | bytes 2098176 | tf_op jit(solution)/shard_map/cos | solution.py:55
  4.2 3.0 %convolution_convert_fusion = bf16[256,2,80,8]{0,2,3,1:T(8,128)(2,1)S(1)} fusion(bf16[80,8,1024]{2,1,0:T(8,128)(2,1)} %param.5, f32[256,1,1024]{2,0,1:T(8,128)S(1)} %get-tuple-element.12, f32[256,1,1024]{2,0,1:T(8,128)S(1)} %get-tuple-element.11), kind=kOutput, calls=%fused_computation.13 | convolution fusion | flops 672989184 | bytes 4063232 | tf_op jit(solution)/shard_map/kct,rst->kcrs/dot_general | solution.py:101
  7.2 0.2 copy.147
  7.4 1.8 copy.95
  9.2 18.4 %all-to-all-start = ((bf16[256,2,640]{2,1,0:T(2,128)(2,1)}), bf16[256,2,640]{2,1,0:T(2,128)(2,1)S(1)}, u32[]{:S(2)}, u32[]{:S(2)}) async-start(bf16[256,2,640]{2,1,0:T(2,128)(2,1)} %copy.95), calls=%async_computation | async-start | bytes 1310720 | tf_op jit(solution)/shard_map/all_to_all | solution.py:116
  27.7 0.1 add.170
  27.9 21.9 %all-to-all-done = bf16[256,2,640]{2,1,0:T(2,128)(2,1)S(1)} async-done(((bf16[256,2,640]{2,1,0:T(2,128)(2,1)}), bf16[256,2,640]{2,1,0:T(2,128)(2,1)S(1)}, u32[]{:S(2)}, u32[]{:S(2)}) %all-to-all-start) | async-done | bytes 655392 | tf_op jit(solution)/shard_map/all_to_all | solution.py:116
  49.8 0.5 copy.128
  50.2 2.8 %broadcast_in_dim.82 = bf16[4,1,2,2,81920]{4,3,2,1,0:T(2,128)(2,1)} broadcast(bf16[2,2,81920]{2,1,0:T(2,128)(2,1)S(1)} %bitcast.120), dimensions={2,3,4} | broadcast | bytes 3276800 | tf_op jit(solution)/shard_map/broadcast_in_dim | solution.py:16
  53.1 4.9 %all-to-all-start.1 = ((bf16[4,1,2,2,81920]{4,3,2,1,0:T(2,128)(2,1)}), bf16[4,1,2,2,81920]{4,3,2,1,0:T(2,128)(2,1)}, u32[]{:S(2)}, u32[]{:S(2)}) async-start(bf16[4,1,2,2,81920]{4,3,2,1,0:T(2,128)(2,1)} %broadcast_in_dim.82), calls=%async_computation.1 | async-start | bytes 5242880 | tf_op jit(solution)/shard_map/all_to_all | solution.py:17
  58.0 1.1 copy.146
  59.1 1.0 pad_bitcast_fusion
  60.1 45.9 %gather_fusion = bf16[5120,2,256]{2,1,0:T(2,128)(2,1)} fusion(bf16[2,2,576,256]{3,1,2,0:T(2,128)(2,1)S(1)} %pad_bitcast_fusion, s32[5120]{0:T(1024)S(1)} %reshape.409), kind=kCustom, calls=%fused_computation | custom fusion | bytes 10526720 | tf_op jit(solution)/shard_map/vmap(jit(_take))/gather | solution.py:68
  106.0 5.5 %copy.99 = bf16[2,2560,2,256]{3,1,2,0:T(8,128)(2,1)} copy(bf16[2,2560,2,256]{3,2,1,0:T(2,128)(2,1)} %bitcast.115) | data formatting | bytes 10485760 | tf_op jit(solution)/shard_map/vmap(jit(_take))/gather | solution.py:68
  111.6 0.1 lt.126
  111.7 0.2 add_reduce_fusion
  111.9 0.1 convert_reduce_fusion
  112.0 0.1 or_bitcast_fusion
  112.1 0.1 fusion.29
  112.2 0.1 iota_compare_fusion.1
  112.3 74.5 %reshape_reshape.6 = bf16[4,2,2,40,256,8]{5,4,3,2,1,0:T(8,128)(2,1)} reshape(bf16[4,1,2,2,81920]{4,3,2,1,0:T(2,128)(2,1)} %all-to-all-done.1) | data formatting | bytes 5242880 | tf_op jit(solution)/shard_map/reshape;reshape | solution.py:119
  186.8 30.3 %copy.97 = bf16[2,2,40,256,4,8]{3,5,4,1,2,0:T(8,128)(2,1)} copy(bf16[2,2,40,256,4,8]{5,3,2,1,0,4:T(8,128)(2,1)} %bitcast.113) | data formatting | bytes 5242880 | tf_op jit(solution)/shard_map/transpose | solution.py:120
  217.1 5.1 %fusion.3 = f32[2,2,2,40,64,32]{4,5,1,2,3,0:T(8,128)S(1)} fusion(bf16[2,2,40,256,4,8]{3,5,4,1,2,0:T(8,128)(2,1)} %copy.97, bf16[2,2,40,64,256]{4,3,2,1,0:T(8,128)(2,1)} %bitcast.116, pred[2,40,64]{2,1,0:T(8,128)(4,1)S(1)} %fusion.29), kind=kOutput, calls=%fused_computation.6 | convolution fusion | flops 338165760 | bytes 10490880 | tf_op jit(solution)/shard_map/afjmr,fbjrs->fabjms/dot_general | solution.py:125
  222.2 0.6 slice_subtract_fusion
  222.8 1.1 copy.101
  223.9 1.5 sub.52
  225.4 1.1 copy.102
  226.5 2.2 add.175
  228.7 1.1 fusion.8
  229.8 4.1 %copy.105 = bf16[2,2,2560,32]{3,1,2,0:T(2,128)(2,1)} copy(bf16[2,2,2560,32]{2,3,1,0:T(8,128)(2,1)S(1)} %fusion.8) | data formatting | bytes 1310720 | tf_op jit(solution)/shard_map/convert_element_type | solution.py:131
  233.9 10.2 %gather_fusion.1 = bf16[1024,2,32]{2,1,0:T(2,128)(2,1)} fusion(bf16[2,2,2560,32]{3,1,2,0:T(2,128)(2,1)} %copy.105, s32[1024]{0:T(1024)S(1)} %bitcast.114), kind=kCustom, calls=%fused_computation.1 | custom fusion | bytes 270336 | tf_op jit(solution)/shard_map/vmap(jit(_take))/gather | solution.py:85
  244.1 1.5 copy.123
  245.6 0.1 fusion.23
  245.7 0.4 convolution_bitcast_fusion.1
  246.2 0.1 copy.110
  246.3 0.1 add.180
  246.4 0.1 copy.109
  246.6 0.1 sub.55
  246.7 0.1 copy.148
  246.9 0.2 reshape.429
  247.0 5.5 %all_to_all.30 = bf16[2,2,8192]{2,1,0:T(2,128)(2,1)S(1)} all-to-all(bf16[2,2,8192]{2,1,0:T(2,128)(2,1)S(1)} %reshape.429), channel_id=1, replica_groups=mesh['freq_0'=8,'freq_1'=8,'freq_2'=2,'rows'=4] {'freq_2'}, dimensions={0} | all-to-all | bytes 131072 | tf_op jit(solution)/shard_map/all_to_all | solution.py:40
  252.5 0.1 reshape.430
  252.7 0.1 copy_bitcast_fusion.2
  252.8 0.2 reshape.431
  252.9 15.0 %all_to_all.31 = bf16[64,2,256]{2,1,0:T(2,128)(2,1)S(1)} all-to-all(bf16[64,2,256]{2,1,0:T(2,128)(2,1)S(1)} %reshape.431), channel_id=1, replica_groups=mesh['freq_0'=8,'freq_1'=8,'freq_2'=2,'rows'=4] {'freq_0','freq_1'}, dimensions={0} | all-to-all | bytes 131072 | tf_op jit(solution)/shard_map/all_to_all | solution.py:40
  267.9 0.1 reshape.432
  268.0 0.1 copy.113
  268.1 1.0 fusion.11
  (24 shorter events, 0.4 us)
Async XLA Ops:
  0.0 245.7 %copy-start = (bf16[2,2,1,256,512]{4,3,2,1,0:T(8,128)(2,1)S(1)}, bf16[2,2,1,256,512]{4,3,2,1,0:T(8,128)(2,1)}, u32[]{:S(2)}) copy-start(bf16[2,2,1,256,512]{4,3,2,1,0:T(8,128)(2,1)} %param.6) | copy-start | bytes 3145732
  4.2 3.0 %copy-start.1 = (f32[256,1,1024]{2,0,1:T(8,128)}, f32[256,1,1024]{2,0,1:T(8,128)S(1)}, u32[]{:S(2)}) copy-start(f32[256,1,1024]{2,0,1:T(8,128)S(1)} %get-tuple-element.12) | copy-start | bytes 3145732
  7.2 20.4 %copy-start.4 = (s32[2,1,40]{2,1,0:T(1,128)S(1)}, s32[2,1,40]{2,1,0:T(1,128)}, u32[]{:S(2)}) copy-start(s32[2,1,40]{2,1,0:T(1,128)} %param.9) | copy-start | bytes 964
  9.2 40.6 %all-to-all-start = ((bf16[256,2,640]{2,1,0:T(2,128)(2,1)}), bf16[256,2,640]{2,1,0:T(2,128)(2,1)S(1)}, u32[]{:S(2)}, u32[]{:S(2)}) async-start(bf16[256,2,640]{2,1,0:T(2,128)(2,1)} %copy.95), calls=%async_computation | async-start | bytes 1310720 | tf_op jit(solution)/shard_map/all_to_all | solution.py:116
  53.1 4.9 %copy-start.3 = (bf16[2,2,1,512,256]{4,3,2,1,0:T(8,128)(2,1)S(1)}, bf16[2,2,1,512,256]{4,3,2,1,0:T(8,128)(2,1)}, u32[]{:S(2)}) copy-start(bf16[2,2,1,512,256]{4,3,2,1,0:T(8,128)(2,1)} %param.7) | copy-start | bytes 3145732
  53.1 59.2 %all-to-all-start.1 = ((bf16[4,1,2,2,81920]{4,3,2,1,0:T(2,128)(2,1)}), bf16[4,1,2,2,81920]{4,3,2,1,0:T(2,128)(2,1)}, u32[]{:S(2)}, u32[]{:S(2)}) async-start(bf16[4,1,2,2,81920]{4,3,2,1,0:T(2,128)(2,1)} %broadcast_in_dim.82), calls=%async_computation.1 | async-start | bytes 5242880 | tf_op jit(solution)/shard_map/all_to_all | solution.py:17
  106.0 5.5 %copy-start.5 = (s32[2,1,40]{2,1,0:T(1,128)S(1)}, s32[2,1,40]{2,1,0:T(1,128)}, u32[]{:S(2)}) copy-start(s32[2,1,40]{2,1,0:T(1,128)} %param.8) | copy-start | bytes 964
  244.1 24.1 %copy-start.2 = (f32[256,1,1024]{2,0,1:T(8,128)S(1)}, f32[256,1,1024]{2,0,1:T(8,128)}, u32[]{:S(2)}) copy-start(f32[256,1,1024]{2,0,1:T(8,128)} %copy-done.1) | copy-start | bytes 3145732
where the time goes:
time: 271 us; the launch traced here: 269 us
  local copies, waits for them, and re-layouts  187 us (69%)
  starting transfers between devices  23.3 us (9%)
  waiting for transfers between devices  21.9 us (8%)
  blocking collectives  20.4 us (8%)
  matrix products  9.44 us (3%)
  other arithmetic  6.73 us (2%)
    another operation x1, local copies, waits for them, and re-layouts, per_device(): portion.reshape(blocks_in, freq_dev, 2, columns, tile_size, src_dev)  74.5 us
    gather x3, local copies, waits for them, and re-layouts, tile_windows(): jnp.take(v_padded, slot_index, axis=1)  51.4 us
    transpose x1, local copies, waits for them, and re-layouts, per_device(): jnp.transpose(spectra, (1, 2, 3, 4, 0, 5))  30.3 us
    all_to_all x1, waiting for transfers between devices, per_device(): lax.all_to_all(spectrum, FREQ, split_axis=0, concat_axis=2, tiled=True)  21.9 us
    all_to_all x2, blocking collectives, turned_blocks(): lax.all_to_all(parts, axes[k], split_axis=k, concat_axis=k, tiled=True)  20.4 us
    all_to_all x1, starting transfers between devices, per_device(): lax.all_to_all(spectrum, FREQ, split_axis=0, concat_axis=2, tiled=True)  18.4 us
    gather x2, local copies, waits for them, and re-layouts, take_slots(): return jnp.take(values, chosen, axis=1)  11.7 us
  transfers between devices with their start and end apart: 2, of which 1 were waited for; matrix products, arithmetic and copies ran while one was open for 20% of the time, Pallas kernels for 0%

commit v1 on v0

v1 whole, which is shorter than its diff:
```python
import functools
import math

import jax
import jax.numpy as jnp
from jax import lax
from jax.experimental import pallas as pl
from jax.experimental.pallas import tpu as pltpu
from jax.sharding import Mesh
from jax.sharding import PartitionSpec as P

FREQ = ("freq_0", "freq_1", "freq_2")
ROWS_FREQ = ("rows", "freq_0", "freq_1", "freq_2")
BF = jnp.bfloat16
F32 = jnp.float32


def tables(freqs, samples):
    row = jnp.arange(2 * freqs, dtype=jnp.int32)
    g, y, kk, c = row // 32, (row // 4) % 8, (row // 2) % 2, row % 2
    k = 2 * (y * 16 + g) + kk
    t = jnp.arange(samples, dtype=jnp.int32)
    phase = ((k + 1)[:, None] * t[None, :]) % samples
    angle = phase.astype(F32) * (2.0 * math.pi / samples)
    value = jnp.where(c[:, None] == 0, jnp.cos(angle), -jnp.sin(angle))
    forward = (value / math.sqrt(samples)).astype(BF)
    inverse = (value / math.sqrt(freqs)).astype(BF)
    inverse = inverse.reshape(128, 4, samples)
    inverse = jnp.transpose(inverse, (1, 0, 2)).reshape(2 * freqs, samples)
    return forward, inverse


def dft_kernel(w_ref, f_ref, out_ref, o_ref):
    for gb in range(4):
        o_ref[gb] = lax.dot_general(
            w_ref[...], f_ref[pl.ds(gb * 128, 128)], (((1,), (1,)), ((), ())), preferred_element_type=F32
        )
    slot = lax.broadcasted_iota(jnp.int32, (16, 128), 1) // 16
    for chunk in range(5):
        for gb in range(4):
            turned = []
            for s in range(8):
                x = o_ref[gb, pl.ds(chunk * 128 + s, 16, stride=8), :]
                turned.append(pltpu.roll(x, 16 * s, axis=1) if s else x)
            for b in range(8):
                acc = turned[(-b) % 8]
                for p in range(1, 8):
                    acc = jnp.where(slot == p, turned[(p - b) % 8], acc)
                out_ref[gb * 4 + b // 2, pl.ds(chunk * 16, 16), pl.ds((b % 2) * 128, 128)] = acc.astype(BF)


def lane_permutation(h, gamma):
    col = lax.broadcasted_iota(jnp.int32, (512, 512), 1)
    row = lax.broadcasted_iota(jnp.int32, (512, 512), 0)
    y_lo, kk, j, c, s = col // 128, (col // 64) % 2, (col // 16) % 4, (col // 8) % 2, col % 8
    p = (s + 2 * gamma + h) % 8
    source = j * 128 + p * 16 + y_lo * 4 + kk * 2 + c
    return jnp.where(row == source, 1.0, 0.0).astype(BF)


def fold_kernel(a_ref, out_ref):
    gamma = (lax.axis_index("freq_1") * 2 + lax.axis_index("freq_2")) % 4
    for h in range(2):
        lanes = pl.ds(h * 128, 128)
        main = jnp.concatenate([a_ref[pl.ds(j * 256, 256), lanes] for j in range(4)], axis=1)
        last = jnp.concatenate([a_ref[pl.ds(1024 + q * 64, 64), lanes] for q in range(4)], axis=1)
        both = jnp.concatenate([main, last], axis=0)
        moved = jnp.dot(both, lane_permutation(h, gamma), preferred_element_type=F32).astype(BF)
        for y in range(4):
            out_ref[h * 4 + y] = moved[:, y * 128 : (y + 1) * 128]


def half_lanes(a, b, kk):
    low = lax.broadcasted_iota(jnp.int32, a.shape, 1) < 64
    if kk == 0:
        return jnp.where(low, a, pltpu.roll(b, 64, axis=1))
    return jnp.where(low, pltpu.roll(a, 64, axis=1), b)


def swapped(b, width):
    lane = lax.broadcasted_iota(jnp.int32, b.shape, 1)
    real = (lane // width) % 2 == 0
    size = b.shape[1]
    return jnp.where(real, -pltpu.roll(b, size - width, axis=1), pltpu.roll(b, width, axis=1))


def tile_kernel(g_ref, v_ref, u_ref, rank_ref, start_ref, out_ref, fifth_ref, acc_ref):
    lane1 = lax.broadcasted_iota(jnp.int32, (512, 128), 1)
    col = lax.broadcasted_iota(jnp.int32, (512, 512), 1)
    row = lax.broadcasted_iota(jnp.int32, (512, 512), 0)
    q, kk_, x_, cs = col // 128, (col // 64) % 2, (col // 16) % 4, col % 16
    perm = jnp.where(row == x_ * 128 + kk_ * 64 + q * 16 + cs, 1.0, 0.0).astype(BF)
    for y in range(8):
        lhs = jnp.concatenate([g_ref[x, y, pl.ds(256, 64), :] for x in range(4)], axis=1)
        moved = jnp.dot(lhs, perm, preferred_element_type=F32)
        for b in range(4):
            fifth_ref[y, pl.ds(b * 64, 64), :] = moved[:, b * 128 : (b + 1) * 128]
    coeffs = []
    tgt = lax.broadcasted_iota(jnp.int32, (256, 128), 1)
    src = lax.broadcasted_iota(jnp.int32, (256, 128), 0)
    for kk in range(2):
        starts = start_ref[kk]
        ranks = rank_ref[kk]
        total = jnp.max(starts + ranks, axis=1, keepdims=True)
        slot40 = lax.broadcasted_iota(jnp.int32, (512, 40), 0)
        begun = jnp.where(starts <= slot40, 1.0, 0.0) + jnp.where(total <= slot40, 64.0, 0.0)
        owner = jnp.sum(begun, axis=1, keepdims=True).astype(jnp.int32) - 1
        v = v_ref[:, kk].reshape(1024, 256)
        acc_ref[...] = jnp.zeros_like(acc_ref)
        for part in range(2):
            if part == 0:
                place = owner - (lane1 // 16) % 4
            else:
                place = owner - 5 * (lane1 // 64)
            for y in range(8 if part == 0 else 2):
                if part == 0:
                    pairs = [(g_ref[2 * m, y, pl.ds(0, 256), :].astype(F32),
                              g_ref[2 * m + 1, y, pl.ds(0, 256), :].astype(F32)) for m in range(2)]
                else:
                    pairs = [(fifth_ref[4 * y + 2 * m], fifth_ref[4 * y + 2 * m + 1]) for m in range(2)]
                rhs = jnp.concatenate([half_lanes(a, b, kk) for a, b in pairs], axis=1).astype(BF)
                prod = jnp.dot(v, rhs, preferred_element_type=F32)
                for m in range(2):
                    lanes = pl.ds(m * 128, 128)
                    if part == 0:
                        hit = place == 5 * y
                    else:
                        hit = place == 5 * (4 * y + 2 * m) + 4
                    for ab in range(2):
                        rows = pl.ds(ab * 512, 512)
                        acc_ref[part, rows, lanes] = jnp.where(
                            hit, prod[ab * 512 : (ab + 1) * 512, m * 128 : (m + 1) * 128], acc_ref[part, rows, lanes]
                        )
        total_c = jnp.zeros((512, 128), F32)
        for part in range(2):
            if part == 0:
                xs, c, s = src // 64, (src // 8) % 2, src % 8
            else:
                xs, c, s = (src // 16) % 4, (src // 8) % 2, src % 8
            join = jnp.where(tgt == kk * 64 + c * 32 + xs * 8 + s, 1.0, 0.0).astype(BF)
            for m in range(2):
                lanes = pl.ds(m * 128, 128)
                value = acc_ref[part, pl.ds(0, 512), lanes] + swapped(acc_ref[part, pl.ds(512, 512), lanes], 8)
                total_c = total_c + jnp.dot(
                    value.astype(BF), join[m * 128 : (m + 1) * 128], preferred_element_type=F32
                )
        coeffs.append(total_c.astype(BF))
    e = jnp.zeros((512, 128), F32)
    for kk in range(2):
        e = e + jnp.dot(u_ref[:, kk].reshape(512, 512), coeffs[kk], preferred_element_type=F32)
    out_ref[...] = (e[:256] + swapped(e[256:], 32)).astype(BF)


VM = pl.BlockSpec(memory_space=pltpu.VMEM)
PARAMS = pltpu.CompilerParams(vmem_limit_bytes=60 * 1024 * 1024)


def per_device(wavefield, u_factors, v_factors, tile_ranks, tile_offsets):
    forward, inverse = tables(256, 1024)
    chunks = pl.pallas_call(
        dft_kernel,
        out_shape=jax.ShapeDtypeStruct((16, 80, 256), BF),
        in_specs=[VM, VM],
        out_specs=VM,
        scratch_shapes=[pltpu.VMEM((4, 640, 128), F32)],
        compiler_params=PARAMS,
    )(wavefield.reshape(640, 1024), forward)
    got = lax.all_to_all(chunks, ("freq_1", "freq_2"), 0, 0, tiled=True)
    folded = pl.pallas_call(
        fold_kernel,
        out_shape=jax.ShapeDtypeStruct((8, 320, 128), BF),
        in_specs=[VM],
        out_specs=VM,
        compiler_params=PARAMS,
    )(got.reshape(1280, 256))
    mine = lax.all_to_all(folded, "freq_0", 0, 0, tiled=True)
    copies = jnp.broadcast_to(mine, (4, *mine.shape))
    gathered = lax.all_to_all(copies, "rows", 0, 0, tiled=True)
    bands = pl.pallas_call(
        tile_kernel,
        out_shape=jax.ShapeDtypeStruct((256, 128), BF),
        in_specs=[VM] * 5,
        out_specs=VM,
        scratch_shapes=[pltpu.VMEM((8, 256, 128), F32), pltpu.VMEM((2, 1024, 256), F32)],
        compiler_params=PARAMS,
    )(gathered, v_factors[:, :, 0], u_factors[:, :, 0], tile_ranks, tile_offsets)
    first = lax.all_to_all(bands.reshape(8, 32, 128), "freq_0", 0, 0, tiled=True)
    first = jnp.transpose(first.reshape(8, 16, 2, 128), (1, 0, 2, 3))
    second = lax.all_to_all(first, ("freq_1", "freq_2"), 0, 0, tiled=True)
    lhs = jnp.transpose(second.reshape(128, 2, 4, 32), (1, 3, 2, 0)).reshape(64, 512)
    series = jnp.dot(lhs, inverse, preferred_element_type=F32)
    return series.astype(BF).reshape(2, 32, 1024)


def solution(mesh):
    torus = Mesh(
        mesh.devices.reshape(8, 8, 2, mesh.shape["rows"]), ("freq_0", "freq_1", "freq_2", "rows")
    )
    return jax.shard_map(
        per_device,
        mesh=torus,
        in_specs=(
            P(FREQ, "rows", None),
            P(None, FREQ, "rows", None, None),
            P(None, FREQ, "rows", None, None),
            P(FREQ, "rows", None),
            P(FREQ, "rows", None),
        ),
        out_specs=P(ROWS_FREQ, None, None),
        check_vma=False,
    )
```

time: 271 us -> 149 us (0.55)
  local copies, waits for them, and re-layouts: 187 us -> 1.55 us
  blocking collectives: 20.4 us -> 94.7 us
  Pallas kernels: 0 us -> 15.5 us
  waiting for transfers between devices: 21.9 us -> 7.21 us
  starting transfers between devices: 23.3 us -> 9.57 us
  other arithmetic: 6.73 us -> 19.2 us
  matrix products: 9.44 us -> 0.96 us
    another operation x3 -> x0, local copies, waits for them, and re-layouts: 74.7 us -> none  [the longest x1 74.5 us: per_device(): portion.reshape(blocks_in, freq_dev, 2, columns, tile_size, src_dev)]
    all_to_all x2 -> x3, blocking collectives: 20.4 us -> 94.7 us  [the longest x1 34.9 us: per_device(): gathered = lax.all_to_all(copies, 'rows', 0, 0, tiled=True)]
    gather x5 -> x0, local copies, waits for them, and re-layouts: 63.1 us -> none  [the longest x3 51.4 us: tile_windows(): jnp.take(v_padded, slot_index, axis=1)]
    transpose x2 -> x1, local copies, waits for them, and re-layouts: 31.2 us -> 0.15 us  [per_device(): jnp.transpose(second.reshape(128, 2, 4, 32), (1, 3, 2, 0)).reshape(64, 512)]
    convert_element_type x1 -> x2, other arithmetic: 1.09 us -> 19.1 us  [the longest x1 9.91 us: tables(): forward = (value / math.sqrt(samples)).astype(BF)]
    pallas_call x0 -> x3, Pallas kernels: none -> 15.5 us  [the longest x1 8.67 us: per_device(): pl.pallas_call(tile_kernel, out_shape=jax.ShapeDtypeStruct((256, 128), BF...]
    all_to_all x2, waiting for transfers between devices: 21.9 us -> 7.21 us  [the longest x1 7.21 us: per_device(): lax.all_to_all(bands.reshape(8, 32, 128), 'freq_0', 0, 0, tiled=True)]
    all_to_all x2, starting transfers between devices: 23.3 us -> 9.57 us  [the longest x1 6.21 us: per_device(): second = lax.all_to_all(first, ('freq_1', 'freq_2'), 0, 0, tiled=True)]
  transfers between devices with their start and end apart: 2 -> 2, of which waited for: 1 -> 1; matrix products, arithmetic and copies ran while one was open for 20% -> 6% of each run, Pallas kernels for 0% -> 0%
where the time goes in v1:
time: 149 us
  blocking collectives  94.7 us (64%)
  other arithmetic  19.2 us (13%)
  Pallas kernels  15.5 us (10%)
  starting transfers between devices  9.57 us (6%)
  waiting for transfers between devices  7.21 us (5%)
  local copies, waits for them, and re-layouts  1.55 us (1%)
    all_to_all x1, blocking collectives, per_device(): gathered = lax.all_to_all(copies, 'rows', 0, 0, tiled=True)  34.9 us
    all_to_all x1, blocking collectives, per_device(): got = lax.all_to_all(chunks, ('freq_1', 'freq_2'), 0, 0, tiled=True)  32.1 us
    all_to_all x1, blocking collectives, per_device(): mine = lax.all_to_all(folded, 'freq_0', 0, 0, tiled=True)  27.6 us
    convert_element_type x1, other arithmetic, tables(): forward = (value / math.sqrt(samples)).astype(BF)  9.91 us
    convert_element_type x1, other arithmetic, tables(): inverse = (value / math.sqrt(freqs)).astype(BF)  9.23 us
    pallas_call x1, Pallas kernels, per_device(): pl.pallas_call(tile_kernel, out_shape=jax.ShapeDtypeStruct((256, 128), BF...  8.67 us
    all_to_all x1, waiting for transfers between devices, per_device(): lax.all_to_all(bands.reshape(8, 32, 128), 'freq_0', 0, 0, tiled=True)  7.21 us
    all_to_all x1, starting transfers between devices, per_device(): second = lax.all_to_all(first, ('freq_1', 'freq_2'), 0, 0, tiled=True)  6.21 us
  transfers between devices with their start and end apart: 2, of which 1 were waited for; matrix products, arithmetic and copies ran while one was open for 6% of the time, Pallas kernels for 0%

profile of v1, /device:TPU:1, one launch (start us, length us, event | category | flops | bytes accessed | tf_op | source)
XLA Modules:
  0.0 148.7 jit_solution(5520218704715464376)
XLA Ops:
  0.0 9.9 %multiply_convert_fusion.1.f_ref = bf16[512,1024]{1,0:T(8,128)(2,1)} fusion(s32[512]{0:T(512)S(1)} %fusion.20, pred[512]{0:T(512)(128)(4,1)S(1)} %fusion.14), kind=kLoop, calls=%fused_computation.15 | loop fusion | flops 9437184 | bytes 1051136 | tf_op jit(solution)/shard_map/convert_element_type | solution.py:26
  9.9 4.3 %shard_map.55 = bf16[16,80,256]{2,1,0:T(8,128)(2,1)} custom-call(bf16[640,1024]{1,0:T(8,128)(2,1)} %bitcast.22, bf16[512,1024]{1,0:T(8,128)(2,1)} %multiply_convert_fusion.1.f_ref), custom_call_target="tpu_custom_call" | custom-call | tf_op jit(solution)/shard_map/pallas_call | solution.py:160
  14.2 32.1 %all_to_all.25 = bf16[16,80,256]{2,1,0:T(8,128)(2,1)} all-to-all(bf16[16,80,256]{2,1,0:T(8,128)(2,1)} %shard_map.55), channel_id=1, replica_groups=mesh['freq_0'=8,'freq_1'=8,'freq_2'=2,'rows'=4] {'freq_1','freq_2'}, dimensions={0} | all-to-all | bytes 1310720 | tf_op jit(solution)/shard_map/all_to_all | solution.py:168
  46.4 2.5 %shard_map.56 = bf16[8,320,128]{2,1,0:T(8,128)(2,1)} custom-call(bf16[1280,256]{1,0:T(8,128)(2,1)} %bitcast.21), custom_call_target="tpu_custom_call" | custom-call | tf_op jit(solution)/shard_map/pallas_call | solution.py:169
  48.8 27.6 %all_to_all.26 = bf16[8,320,128]{2,1,0:T(8,128)(2,1)S(1)} all-to-all(bf16[8,320,128]{2,1,0:T(8,128)(2,1)} %shard_map.56), channel_id=1, replica_groups=mesh['freq_0'=8,'freq_1'=8,'freq_2'=2,'rows'=4] {'freq_0'}, dimensions={0} | all-to-all | bytes 1310720 | tf_op jit(solution)/shard_map/all_to_all | solution.py:176
  76.5 0.6 broadcast_in_dim.17
  77.1 34.9 %all_to_all.27.g_ref = bf16[4,8,320,128]{3,2,1,0:T(8,128)(2,1)} all-to-all(bf16[4,8,320,128]{3,2,1,0:T(8,128)(2,1)S(1)} %broadcast_in_dim.17), channel_id=1, replica_groups=mesh['freq_0'=8,'freq_1'=8,'freq_2'=2,'rows'=4] {'rows'}, dimensions={0} | all-to-all | bytes 5242880 | tf_op jit(solution)/shard_map/all_to_all | solution.py:178
  112.0 8.7 %shard_map.57 = bf16[256,128]{1,0:T(8,128)(2,1)} custom-call(bf16[4,8,320,128]{3,2,1,0:T(8,128)(2,1)} %all_to_all.27.g_ref, bf16[2,2,512,256]{3,2,1,0:T(8,128)(2,1)} %bitcast.25, bf16[2,2,256,512]{3,2,1,0:T(8,128)(2,1)} %bitcast.26, s32[2,1,40]{2,1,0:T(1,128)} %rank_ref.1, s32[2,1,40]{2,1,0:T(1,128)} %start_ref.1), custom_call_target="tpu_custom_call" | custom-call | tf_op jit(solution)/shard_map/pallas_call | solution.py:179
  120.7 3.4 %all-to-all-start.3 = ((bf16[8,32,128]{2,1,0:T(8,128)(2,1)}), bf16[8,32,128]{2,1,0:T(8,128)(2,1)S(1)}, u32[]{:S(2)}, u32[]{:S(2)}) async-start(bf16[8,32,128]{2,1,0:T(8,128)(2,1)} %bitcast.27), calls=%async_computation.3 | async-start | bytes 131072 | tf_op jit(solution)/shard_map/all_to_all | solution.py:187
  124.1 7.2 %all-to-all-done.3 = bf16[8,32,128]{2,1,0:T(8,128)(2,1)S(1)} async-done(((bf16[8,32,128]{2,1,0:T(8,128)(2,1)}), bf16[8,32,128]{2,1,0:T(8,128)(2,1)S(1)}, u32[]{:S(2)}, u32[]{:S(2)}) %all-to-all-start.3) | async-done | bytes 65568 | tf_op jit(solution)/shard_map/all_to_all | solution.py:187
  131.3 0.7 copy.10
  131.9 6.2 %all-to-all-start.4 = ((bf16[16,8,2,128]{3,1,2,0:T(8,128)(2,1)}), bf16[16,8,2,128]{3,1,2,0:T(8,128)(2,1)S(1)}, u32[]{:S(2)}, u32[]{:S(2)}) async-start(bf16[16,8,2,128]{3,1,2,0:T(8,128)(2,1)} %bitcast.6), calls=%async_computation.4 | async-start | bytes 131072 | tf_op jit(solution)/shard_map/all_to_all | solution.py:189
  138.1 9.2 %multiply_convert_fusion = bf16[4,128,1024]{2,1,0:T(8,128)(2,1)S(1)} fusion(s32[4,128]{1,0:T(4,128)S(1)} %fusion.28, pred[4,128]{1,0:T(4,128)(4,1)S(1)} %fusion.22), kind=kLoop, calls=%fused_computation.12 | loop fusion | flops 9437184 | bytes 1051136 | tf_op jit(solution)/shard_map/convert_element_type | solution.py:27
  147.4 0.0 all-to-all-done.4
  147.4 0.2 reshape.157
  147.6 0.2 copy.12
  147.7 1.0 convolution_convert_fusion
  (5 shorter events, 0.1 us)
Async XLA Ops:
  120.7 10.6 %all-to-all-start.3 = ((bf16[8,32,128]{2,1,0:T(8,128)(2,1)}), bf16[8,32,128]{2,1,0:T(8,128)(2,1)S(1)}, u32[]{:S(2)}, u32[]{:S(2)}) async-start(bf16[8,32,128]{2,1,0:T(8,128)(2,1)} %bitcast.27), calls=%async_computation.3 | async-start | bytes 131072 | tf_op jit(solution)/shard_map/all_to_all | solution.py:187
  131.9 15.5 %all-to-all-start.4 = ((bf16[16,8,2,128]{3,1,2,0:T(8,128)(2,1)}), bf16[16,8,2,128]{3,1,2,0:T(8,128)(2,1)S(1)}, u32[]{:S(2)}, u32[]{:S(2)}) async-start(bf16[16,8,2,128]{3,1,2,0:T(8,128)(2,1)} %bitcast.6), calls=%async_computation.4 | async-start | bytes 131072 | tf_op jit(solution)/shard_map/all_to_all | solution.py:189

commit v2 on v0

v2 whole, which is shorter than its diff:
```python
import math

import jax
import jax.numpy as jnp
import numpy as np
from jax import lax
from jax.experimental import pallas as pl
from jax.experimental.pallas import tpu as pltpu
from jax.sharding import Mesh
from jax.sharding import PartitionSpec as P

FREQ = ("freq_0", "freq_1", "freq_2")
ROWS_FREQ = ("rows", "freq_0", "freq_1", "freq_2")
BF = jnp.bfloat16
F32 = jnp.float32
MESH = pl.DeviceIdType.MESH

_z = 0.125 * (1.0 - np.cos(np.pi * (np.arange(64) + 0.5) / 64))
COS = [float(a) for a in np.polynomial.polynomial.polyfit(_z, np.cos(2 * np.pi * np.sqrt(_z)), 9)]

STEPS = [(0, 1)] + [(d, c) for n in (1, 2, 3) for d in (n, 8 - n) for c in (0, 1)] + [(4, 0), (4, 1)]
YSTEPS = (1, 7, 2, 6, 3, 5, 4)


def cosine(m):
    x = jnp.where(m >= 512, m - 1024, m).astype(F32) * (1.0 / 1024.0)
    z = x * x
    value = jnp.full(m.shape, COS[-1], F32)
    for a in COS[-2::-1]:
        value = value * z + a
    return value


def build_table(f_ref, kk):
    for part in range(4):
        row = lax.broadcasted_iota(jnp.int32, (64, 128), 0) + part * 64
        lane = lax.broadcasted_iota(jnp.int32, (64, 128), 1)
        k1 = (row // 2) * 2 + (kk + 1)
        m = (k1 * lane + (row % 2) * 256) & 1023
        co, si = cosine(m), cosine((m + 768) & 1023)
        turn = (k1 * 128) & 1023
        ct, st = cosine(turn), cosine((turn + 768) & 1023)
        for b in range(8):
            f_ref[kk, pl.ds(part * 64, 64), pl.ds(b * 128, 128)] = (co * (1.0 / 32.0)).astype(BF)
            if b < 7:
                co, si = co * ct - si * st, si * ct + co * st


def one_hot(shape, source):
    row = lax.broadcasted_iota(jnp.int32, shape, 0)
    return jnp.where(row == source, 1.0, 0.0).astype(BF)


def swapped(b, width):
    lane = lax.broadcasted_iota(jnp.int32, b.shape, 1)
    real = (lane // width) % 2 == 0
    return jnp.where(real, -pltpu.roll(b, b.shape[1] - width, axis=1), pltpu.roll(b, width, axis=1))


def kernel(
    w_hbm, v_hbm, u_hbm, rank_ref, start_ref, out_ref,
    w, v, u, f, o, s1, r1, perm, p2, g, place, acc, table, bb, ry, pz, rz,
    load_sem, s1s, r1s, p2s, p2r, xs, xm, xp, x2, xs2, f1s, f1r, f2s, f2r,
):
    y = lax.axis_index("freq_0")
    z = lax.axis_index("freq_1")
    core = lax.axis_index("freq_2")
    x = lax.axis_index("rows")
    me_g = z * 2 + core

    loads = [pltpu.make_async_copy(w_hbm, w, load_sem.at[0])]
    for kk in range(2):
        loads.append(pltpu.make_async_copy(v_hbm.at[:, kk], v.at[kk], load_sem.at[1 + kk]))
        loads.append(pltpu.make_async_copy(u_hbm.at[:, kk], u.at[kk], load_sem.at[3 + kk]))
    for load in loads:
        load.start()

    def y_peer(d):
        return {"freq_0": (y + d) % 8}

    def g_peer(d):
        return {"freq_1": (z + d[0]) % 8, "freq_2": (core + d[1]) % 2}

    def g_to(d):
        return ((z + d[0]) % 8) * 2 + (core + d[1]) % 2

    def g_from(d):
        return ((z + 8 - d[0]) % 8) * 2 + (core + 2 - d[1]) % 2

    x_up, x_down = (x + 1) % 4, (x + 3) % 4

    barrier = pltpu.get_barrier_semaphore()
    for d in YSTEPS:
        pl.semaphore_signal(barrier, inc=1, device_id=y_peer(d), device_id_type=MESH)
    for d in STEPS:
        pl.semaphore_signal(barrier, inc=1, device_id=g_peer(d), device_id_type=MESH)
    for peer in (x_up, x_down):
        pl.semaphore_signal(barrier, inc=1, device_id={"rows": peer}, device_id_type=MESH)

    def send(src, dst, ssem, rsem, peer):
        return pltpu.make_async_remote_copy(
            src_ref=src, dst_ref=dst, send_sem=ssem, recv_sem=rsem, device_id=peer, device_id_type=MESH
        )

    def y_copy(kk, i):
        d = YSTEPS[i]
        return send(s1.at[kk, (y + d) % 8], r1.at[kk, y], s1s.at[kk, i], r1s.at[kk, i], y_peer(d))

    def g_copy(kk, i):
        d = STEPS[i]
        rows = pl.ds(me_g * 80, 80)
        return send(p2.at[kk, g_to(d)], g.at[x, kk, rows], p2s.at[kk, i], p2r.at[kk, i], g_peer(d))

    def block(kk, i, owner):
        gs = me_g if i == 0 else g_from(STEPS[i - 1])
        return g.at[owner, kk, pl.ds(gs * 80, 80)]

    def x_copy(kk, i, up):
        ref = block(kk, i, x)
        if up:
            return send(ref, ref, xs.at[kk, 0], xm.at[kk, i], {"rows": x_up})
        return send(ref, ref, xs.at[kk, 1], xp.at[kk, i], {"rows": x_down})

    def x_relay(kk, i):
        if i % 2 == 0:
            ref = block(kk, i, x_down)
            return send(ref, ref, xs2.at[kk, 0], x2.at[kk], {"rows": x_up})
        ref = block(kk, i, x_up)
        return send(ref, ref, xs2.at[kk, 1], x2.at[kk], {"rows": x_down})

    def dft(kk):
        for half in range(2):
            o[half] = lax.dot_general(
                w[...], f[kk, pl.ds(half * 128, 128)], (((1,), (1,)), ((), ())), preferred_element_type=F32
            )
        slot = lax.broadcasted_iota(jnp.int32, (16, 128), 1) // 16

        def place_rows(chunk, carry):
            for half in range(2):
                turned = []
                for s in range(8):
                    t = o[half, pl.ds(chunk * 128 + s, 16, stride=8), :]
                    turned.append(pltpu.roll(t, 16 * s, axis=1) if s else t)
                for b in range(8):
                    value = turned[(-b) % 8]
                    for q in range(1, 8):
                        value = jnp.where(slot == q, turned[(q - b) % 8], value)
                    rows = pl.ds(pl.multiple_of(chunk * 16, 16), 16)
                    s1[kk, half * 4 + b // 2, rows, pl.ds((b % 2) * 128, 128)] = value.astype(BF)
            return carry

        lax.fori_loop(0, 5, place_rows, 0)

    def y_send(kk):
        for i in range(7):
            y_copy(kk, i).start()
        r1[kk, y] = s1[kk, y]

    def g_send(kk):
        for i in range(7):
            y_copy(kk, i).wait_recv()
        lhs = jnp.concatenate(
            [
                jnp.concatenate([r1[kk, a, :, pl.ds(h * 128, 128)] for a in range(8)], axis=1)
                for h in range(2)
            ],
            axis=0,
        )
        for b in range(8):
            moved = jnp.dot(lhs, perm[:, pl.ds(b * 128, 128)], preferred_element_type=F32).astype(BF)
            p2[kk, b] = moved[:80]
            p2[kk, 8 + b] = moved[80:]
        for i in range(15):
            g_copy(kk, i).start()
        g[x, kk, pl.ds(pl.multiple_of(me_g * 80, 16), 80)] = p2[kk, me_g]

    def forward(kk, i):
        if i > 0:
            g_copy(kk, i - 1).wait_recv()
        x_copy(kk, i, True).start()
        x_copy(kk, i, False).start()

    def relay(kk, i):
        x_copy(kk, i, True).wait_recv()
        x_copy(kk, i, False).wait_recv()
        x_relay(kk, i).start()

    def whole(kk, owner, ssem, rsem, rows=1280):
        ref = g.at[owner, kk, pl.ds(0, rows)]
        return send(ref, ref, ssem, rsem, {"rows": x_up})

    def settle(kk):
        whole(kk, x, xs.at[kk, 0], x2.at[kk]).wait_recv()

    def products(kk, jj):
        for half in range(2):
            rows = pl.ds(jj * 256, 256)
            rhs = jnp.concatenate([g[2 * half, kk, rows, :], g[2 * half + 1, kk, rows, :]], axis=1)
            prod = jnp.dot(v[kk].reshape(1024, 256), rhs, preferred_element_type=F32)
            for m in range(2):
                hit = place[kk] == jj
                lanes = pl.ds((2 * half + m) * 128, 128)
                for ab in range(2):
                    old = acc[pl.ds(ab * 512, 512), lanes] if jj else 0.0
                    new = prod[ab * 512 : (ab + 1) * 512, m * 128 : (m + 1) * 128]
                    acc[pl.ds(ab * 512, 512), lanes] = jnp.where(hit, new, old)

    def coefficients(kk):
        turn = (y % 4) * 2 + z // 4
        row = lax.broadcasted_iota(jnp.int32, (128, 128), 0)
        col = lax.broadcasted_iota(jnp.int32, (128, 128), 1)
        c, s = (row // 8) % 2, (row % 8 + 8 - turn) % 8
        total = jnp.zeros((512, 128), F32)
        for b in range(4):
            lanes = pl.ds(b * 128, 128)
            value = acc[pl.ds(0, 512), lanes] + swapped(acc[pl.ds(512, 512), lanes], 8)
            join = jnp.where(col == kk * 64 + c * 32 + b * 8 + s, 1.0, 0.0).astype(BF)
            total = total + jnp.dot(value.astype(BF), join, preferred_element_type=F32)
        return jnp.dot(u[kk].reshape(512, 512), total.astype(BF), preferred_element_type=F32)

    build_table(f, 0)
    loads[0].wait()
    dft(0)
    pl.semaphore_wait(barrier, 24)
    y_send(0)
    build_table(f, 1)
    dft(1)
    y_send(1)

    col = lax.broadcasted_iota(jnp.int32, (1024, 128), 1)
    for b in range(8):
        perm[:, pl.ds(b * 128, 128)] = one_hot(
            (1024, 128), (col // 16) * 128 + (col % 8) * 16 + b * 2 + (col // 8) % 2
        )
    lane = lax.broadcasted_iota(jnp.int32, (512, 128), 1)
    slot40 = lax.broadcasted_iota(jnp.int32, (512, 40), 0)
    for kk in range(2):
        starts = start_ref[kk]
        total = jnp.max(starts + rank_ref[kk], axis=1, keepdims=True)
        begun = jnp.where(starts <= slot40, 1.0, 0.0) + jnp.where(total <= slot40, 64.0, 0.0)
        owner = jnp.sum(begun, axis=1, keepdims=True).astype(jnp.int32) - 1
        place[kk] = owner - 5 * (lane // 16)
    n = lax.broadcasted_iota(jnp.int32, (256, 256), 0)
    col = lax.broadcasted_iota(jnp.int32, (256, 256), 1)
    for c in range(2):
        source = ((n % 8) * 16 + n // 16) * 2 + c
        pick = jnp.where(col == source, 2.0, 0.0).astype(BF)
        for kk in range(2):
            table[kk * 2 + c] = jnp.dot(pick, f[kk], preferred_element_type=F32).astype(BF)

    g_send(0)
    for i in range(8):
        forward(0, i)
        if i >= 4:
            relay(0, i - 4)
    g_send(1)
    for i in range(8, 16):
        forward(0, i)
        relay(0, i - 4)
    for i in range(4):
        forward(1, i)
        relay(0, 12 + i)
    settle(0)
    for load in loads[1:]:
        load.wait()
    for jj in range(5):
        products(0, jj)
        for i in range(4 + 2 * jj, 6 + 2 * jj):
            forward(1, i)
            relay(1, i - 4)
    for i in range(14, 16):
        forward(1, i)
        relay(1, i - 4)
    e = coefficients(0)
    for i in range(12, 16):
        relay(1, i)
    settle(1)
    for jj in range(5):
        products(1, jj)
    e = e + coefficients(1)
    bb[...] = (e[:256] + swapped(e[256:], 32)).astype(BF)

    def y_back(i):
        d = YSTEPS[i]
        rows = pl.ds(pl.multiple_of(((y + d) % 8) * 32, 32), 32)
        return send(bb.at[rows], ry.at[y], f1s.at[i], f1r.at[i], y_peer(d))

    def g_back(i):
        d = STEPS[i]
        return send(pz.at[g_to(d)], rz.at[me_g], f2s.at[i], f2r.at[i], g_peer(d))

    for i in range(7):
        y_back(i).start()
    ry[y] = bb[pl.ds(pl.multiple_of(y * 32, 32), 32)]
    source = (n % 8) * 32 + (n // 16) * 2 + (n // 8) % 2
    pick = jnp.where(col == source, 1.0, 0.0).astype(BF)
    for i in range(7):
        y_back(i).wait_recv()
    moved = jnp.dot(pick, ry[...].reshape(256, 128), preferred_element_type=F32)
    pz[...] = moved.astype(BF).reshape(16, 16, 128)
    for i in range(15):
        g_back(i).start()
    rz[me_g] = pz[me_g]
    for i in range(15):
        g_back(i).wait_recv()
    turned = jnp.transpose(rz[...].reshape(256, 128).astype(F32))
    lane = lax.broadcasted_iota(jnp.int32, (32, 256), 1)
    series = jnp.zeros((64, 1024), F32)
    for b in range(4):
        part = turned[b * 32 : (b + 1) * 32]
        lhs = jnp.concatenate([jnp.where((lane // 8) % 2 == q, part, 0.0) for q in range(2)], axis=0)
        series = series + jnp.dot(lhs.astype(BF), table[b], preferred_element_type=F32)
    out_ref[...] = series.astype(BF)

    for kk in range(2):
        for i in range(7):
            y_copy(kk, i).wait_send()
        for i in range(15):
            g_copy(kk, i).wait_send()
        for a in range(2):
            whole(kk, x, xs.at[kk, a], x2.at[kk]).wait_send()
            whole(kk, x, xs2.at[kk, a], x2.at[kk], 640).wait_send()
    for i in range(7):
        y_back(i).wait_send()
    for i in range(15):
        g_back(i).wait_send()


VM = pl.BlockSpec(memory_space=pltpu.VMEM)
ANY = pl.BlockSpec(memory_space=pl.ANY)
DMA = pltpu.SemaphoreType.DMA


def per_device(wavefield, u_factors, v_factors, tile_ranks, tile_offsets):
    series = pl.pallas_call(
        kernel,
        out_shape=jax.ShapeDtypeStruct((64, 1024), BF),
        in_specs=[ANY, ANY, ANY, VM, VM],
        out_specs=VM,
        scratch_shapes=[
            pltpu.VMEM((640, 1024), BF),
            pltpu.VMEM((2, 2, 512, 256), BF),
            pltpu.VMEM((2, 2, 256, 512), BF),
            pltpu.VMEM((2, 256, 1024), BF),
            pltpu.VMEM((2, 640, 128), F32),
            pltpu.VMEM((2, 8, 80, 256), BF),
            pltpu.VMEM((2, 8, 80, 256), BF),
            pltpu.VMEM((1024, 1024), BF),
            pltpu.VMEM((2, 16, 80, 128), BF),
            pltpu.VMEM((4, 2, 1280, 128), BF),
            pltpu.VMEM((2, 512, 128), jnp.int32),
            pltpu.VMEM((1024, 512), F32),
            pltpu.VMEM((4, 256, 1024), BF),
            pltpu.VMEM((256, 128), BF),
            pltpu.VMEM((8, 32, 128), BF),
            pltpu.VMEM((16, 16, 128), BF),
            pltpu.VMEM((16, 16, 128), BF),
            DMA((5,)),
            DMA((2, 7)),
            DMA((2, 7)),
            DMA((2, 15)),
            DMA((2, 15)),
            DMA((2, 2)),
            DMA((2, 16)),
            DMA((2, 16)),
            DMA((2,)),
            DMA((2, 2)),
            DMA((7,)),
            DMA((7,)),
            DMA((15,)),
            DMA((15,)),
        ],
        compiler_params=pltpu.CompilerParams(
            collective_id=0, has_side_effects=True, vmem_limit_bytes=56 * 1024 * 1024
        ),
    )(wavefield.reshape(640, 1024), v_factors[:, :, 0], u_factors[:, :, 0], tile_ranks[:, 0:1], tile_offsets[:, 0:1])
    return series.reshape(2, 32, 1024)


def solution(mesh):
    torus = Mesh(
        mesh.devices.reshape(8, 8, 2, mesh.shape["rows"]), ("freq_0", "freq_1", "freq_2", "rows")
    )
    return jax.shard_map(
        per_device,
        mesh=torus,
        in_specs=(
            P(FREQ, "rows", None),
            P(None, FREQ, "rows", None, None),
            P(None, FREQ, "rows", None, None),
            P(FREQ, "rows", None),
            P(FREQ, "rows", None),
        ),
        out_specs=P(ROWS_FREQ, None, None),
        check_vma=False,
    )
```

time: 271 us -> 80.1 us (0.30)
  local copies, waits for them, and re-layouts: 187 us -> 1.57 us
  Pallas kernels: 0 us -> 78.4 us
  starting transfers between devices: 23.3 us -> 0 us
  waiting for transfers between devices: 21.9 us -> 0 us
  blocking collectives: 20.4 us -> 0 us
  matrix products: 9.44 us -> 0 us
  other arithmetic: 6.73 us -> 0 us
    pallas_call x0 -> x1, Pallas kernels: none -> 78.4 us  [per_device(): pl.pallas_call(kernel, out_shape=jax.ShapeDtypeStruct((64, 1024), BF), in...]
    another operation x3 -> x0, local copies, waits for them, and re-layouts: 74.7 us -> none  [the longest x1 74.5 us: per_device(): portion.reshape(blocks_in, freq_dev, 2, columns, tile_size, src_dev)]
    gather x5 -> x0, local copies, waits for them, and re-layouts: 63.1 us -> none  [the longest x3 51.4 us: tile_windows(): jnp.take(v_padded, slot_index, axis=1)]
    transpose x2 -> x0, local copies, waits for them, and re-layouts: 31.2 us -> none  [the longest x1 30.3 us: per_device(): jnp.transpose(spectra, (1, 2, 3, 4, 0, 5))]
    all_to_all x2 -> x0, starting transfers between devices: 23.3 us -> none  [the longest x1 18.4 us: per_device(): lax.all_to_all(spectrum, FREQ, split_axis=0, concat_axis=2, tiled=True)]
    all_to_all x2 -> x0, waiting for transfers between devices: 21.9 us -> none  [the longest x1 21.9 us: per_device(): lax.all_to_all(spectrum, FREQ, split_axis=0, concat_axis=2, tiled=True)]
    all_to_all x2 -> x0, blocking collectives: 20.4 us -> none  [turned_blocks(): lax.all_to_all(parts, axes[k], split_axis=k, concat_axis=k, tiled=True)]
    dot_general x4 -> x0, matrix products: 9.44 us -> none  [the longest x1 5.07 us: per_device(): jnp.einsum('afjmr,fbjrs->fabjms', v_win, spectra, preferred_element_type=...]
  transfers between devices with their start and end apart: 2 -> 0, of which waited for: 1 -> 0; matrix products, arithmetic and copies ran while one was open for 20% -> 0% of each run, Pallas kernels for 0% -> 0%
where the time goes in v2:
time: 80.1 us; the launch traced here: 80 us
  Pallas kernels  78.4 us (98%)
  local copies, waits for them, and re-layouts  1.57 us (2%)
    pallas_call x1, Pallas kernels, per_device(): pl.pallas_call(kernel, out_shape=jax.ShapeDtypeStruct((64, 1024), BF), in...  78.4 us

profile of v2, /device:TPU:1, one launch (start us, length us, event | category | flops | bytes accessed | tf_op | source)
XLA Modules:
  0.0 80.0 jit_solution(12036763307788910247)
XLA Ops:
  0.0 78.4 %shard_map.55 = bf16[64,1024]{1,0:T(8,128)(2,1)} custom-call(bf16[640,1024]{1,0:T(8,128)(2,1)} %bitcast.4, bf16[2,2,512,256]{3,2,1,0:T(8,128)(2,1)} %bitcast.5, bf16[2,2,256,512]{3,2,1,0:T(8,128)(2,1)} %bitcast.6, s32[2,1,40]{2,1,0:T(1,128)} %rank_ref.1, s32[2,1,40]{2,1,0:T(1,128)} %start_ref.1), custom_call_target="tpu_custom_call" | custom-call | tf_op jit(solution)/shard_map/pallas_call | solution.py:335
  78.4 1.6 %copy.7 = bf16[2,32,1024]{2,1,0:T(8,128)(2,1)} copy(bf16[2,32,1024]{2,1,0:T(8,128)(2,1)} %bitcast.7) | data formatting | bytes 262144

commit v3 on v2

--- a/solution.py
+++ b/solution.py
@@ -18,8 +18,8 @@
 _z = 0.125 * (1.0 - np.cos(np.pi * (np.arange(64) + 0.5) / 64))
 COS = [float(a) for a in np.polynomial.polynomial.polyfit(_z, np.cos(2 * np.pi * np.sqrt(_z)), 9)]
 
-STEPS = [(0, 1)] + [(d, c) for n in (1, 2, 3) for d in (n, 8 - n) for c in (0, 1)] + [(4, 0), (4, 1)]
-YSTEPS = (1, 7, 2, 6, 3, 5, 4)
+STEPS = [(0, 1)] + [(d, c) for d in (1, 7, 4, 3, 5, 2, 6) for c in (0, 1)]
+YSTEPS = (4, 3, 5, 2, 6, 1, 7)
 
 
 def cosine(m):
@@ -59,8 +59,10 @@
 
 def kernel(
     w_hbm, v_hbm, u_hbm, rank_ref, start_ref, out_ref,
-    w, v, u, f, o, s1, r1, perm, p2, g, place, acc, table, bb, ry, pz, rz,
+    w, v, vg, u, f, o, s1, r1, perm, pack, unpack, p2, g, mine, meta, place, place4, acc, cs, cr,
+    table, bb, ry, pz, rz,
     load_sem, s1s, r1s, p2s, p2r, xs, xm, xp, x2, xs2, f1s, f1r, f2s, f2r,
+    vs, vm, vp, v2, vs2, ms, mr, css, crs,
 ):
     y = lax.axis_index("freq_0")
     z = lax.axis_index("freq_1")
@@ -68,10 +70,13 @@
     x = lax.axis_index("rows")
     me_g = z * 2 + core
 
-    loads = [pltpu.make_async_copy(w_hbm, w, load_sem.at[0])]
-    for kk in range(2):
-        loads.append(pltpu.make_async_copy(v_hbm.at[:, kk], v.at[kk], load_sem.at[1 + kk]))
-        loads.append(pltpu.make_async_copy(u_hbm.at[:, kk], u.at[kk], load_sem.at[3 + kk]))
+    loads = [
+        pltpu.make_async_copy(w_hbm, w, load_sem.at[0]),
+        pltpu.make_async_copy(v_hbm.at[:, 1], vg.at[x], load_sem.at[1]),
+        pltpu.make_async_copy(v_hbm.at[:, 0], v, load_sem.at[2]),
+        pltpu.make_async_copy(u_hbm.at[:, 0], u.at[0], load_sem.at[3]),
+        pltpu.make_async_copy(u_hbm.at[:, 1], u.at[1], load_sem.at[4]),
+    ]
     for load in loads:
         load.start()
 
@@ -94,7 +99,7 @@
         pl.semaphore_signal(barrier, inc=1, device_id=y_peer(d), device_id_type=MESH)
     for d in STEPS:
         pl.semaphore_signal(barrier, inc=1, device_id=g_peer(d), device_id_type=MESH)
-    for peer in (x_up, x_down):
+    for peer in (x_up, x_down, (x + 2) % 4):
         pl.semaphore_signal(barrier, inc=1, device_id={"rows": peer}, device_id_type=MESH)
 
     def send(src, dst, ssem, rsem, peer):
@@ -127,6 +132,34 @@
             return send(ref, ref, xs2.at[kk, 0], x2.at[kk], {"rows": x_up})
         ref = block(kk, i, x_up)
         return send(ref, ref, xs2.at[kk, 1], x2.at[kk], {"rows": x_down})
+
+    def v_copy(a, up):
+        ref = vg.at[x, a // 2, pl.ds((a % 2) * 256, 256)]
+        if up:
+            return send(ref, ref, vs.at[0], vm.at[a], {"rows": x_up})
+        return send(ref, ref, vs.at[1], vp.at[a], {"rows": x_down})
+
+    def v_relay(a):
+        rows = pl.ds((a % 2) * 256, 256)
+        if a < 2:
+            ref = vg.at[x_down, a // 2, rows]
+            return send(ref, ref, vs2.at[0], v2, {"rows": x_up})
+        ref = vg.at[x_up, a // 2, rows]
+        return send(ref, ref, vs2.at[1], v2, {"rows": x_down})
+
+    def v_pass(a):
+        v_copy(a, a < 2).wait_recv()
+        v_relay(a).start()
+
+    def meta_copy(d):
+        return send(mine, meta.at[x], ms.at[d - 1], mr.at[d - 1], {"rows": (x + d) % 4})
+
+    def coeff_copy(d):
+        return send(cs.at[(x + d) % 4], cr.at[x], css.at[d - 1], crs.at[d - 1], {"rows": (x + d) % 4})
+
+    def v_whole(ssem, rsem, part):
+        ref = vg.at[x] if part is None else vg.at[x, part]
+        return send(ref, ref, ssem, rsem, {"rows": x_up})
 
     def dft(kk):
         for half in range(2):
@@ -181,8 +214,7 @@
         x_copy(kk, i, False).start()
 
     def relay(kk, i):
-        x_copy(kk, i, True).wait_recv()
-        x_copy(kk, i, False).wait_recv()
+        x_copy(kk, i, i % 2 == 0).wait_recv()
         x_relay(kk, i).start()
 
     def whole(kk, owner, ssem, rsem, rows=1280):
@@ -190,23 +222,24 @@
         return send(ref, ref, ssem, rsem, {"rows": x_up})
 
     def settle(kk):
+        for i in range(16):
+            x_copy(kk, i, i % 2 == 1).wait_recv()
         whole(kk, x, xs.at[kk, 0], x2.at[kk]).wait_recv()
 
-    def products(kk, jj):
+    def products(jj):
         for half in range(2):
             rows = pl.ds(jj * 256, 256)
-            rhs = jnp.concatenate([g[2 * half, kk, rows, :], g[2 * half + 1, kk, rows, :]], axis=1)
-            prod = jnp.dot(v[kk].reshape(1024, 256), rhs, preferred_element_type=F32)
+            rhs = jnp.concatenate([g[2 * half, 0, rows, :], g[2 * half + 1, 0, rows, :]], axis=1)
+            prod = jnp.dot(v[...].reshape(1024, 256), rhs, preferred_element_type=F32)
             for m in range(2):
-                hit = place[kk] == jj
+                hit = place[...] == jj
                 lanes = pl.ds((2 * half + m) * 128, 128)
                 for ab in range(2):
                     old = acc[pl.ds(ab * 512, 512), lanes] if jj else 0.0
                     new = prod[ab * 512 : (ab + 1) * 512, m * 128 : (m + 1) * 128]
                     acc[pl.ds(ab * 512, 512), lanes] = jnp.where(hit, new, old)
 
-    def coefficients(kk):
-        turn = (y % 4) * 2 + z // 4
+    def coefficients():
         row = lax.broadcasted_iota(jnp.int32, (128, 128), 0)
         col = lax.broadcasted_iota(jnp.int32, (128, 128), 1)
         c, s = (row // 8) % 2, (row % 8 + 8 - turn) % 8
@@ -214,15 +247,58 @@
         for b in range(4):
             lanes = pl.ds(b * 128, 128)
             value = acc[pl.ds(0, 512), lanes] + swapped(acc[pl.ds(512, 512), lanes], 8)
-            join = jnp.where(col == kk * 64 + c * 32 + b * 8 + s, 1.0, 0.0).astype(BF)
+            join = jnp.where(col == c * 32 + b * 8 + s, 1.0, 0.0).astype(BF)
             total = total + jnp.dot(value.astype(BF), join, preferred_element_type=F32)
-        return jnp.dot(u[kk].reshape(512, 512), total.astype(BF), preferred_element_type=F32)
+        return total.astype(BF)
+
+    def own_products():
+        lhs = []
+        for row in range(4):
+            factors = vg[row].reshape(1024, 256)
+            for pair in ((0, 1), (2, 3), (4,)):
+                rhs = jnp.concatenate([g[x, 1, pl.ds(jj * 256, 256), :] for jj in pair], axis=1)
+                prod = jnp.dot(factors, rhs, preferred_element_type=F32)
+                for m, jj in enumerate(pair):
+                    hit = place4[row] == jj
+                    for ab in range(2):
+                        rows = pl.ds(ab * 512, 512)
+                        old = acc[rows, pl.ds(row * 128, 128)] if jj else 0.0
+                        new = prod[ab * 512 : (ab + 1) * 512, m * 128 : (m + 1) * 128]
+                        acc[rows, pl.ds(row * 128, 128)] = jnp.where(hit, new, old)
+            lanes = pl.ds(row * 128, 128)
+            value = (acc[pl.ds(0, 512), lanes] + swapped(acc[pl.ds(512, 512), lanes], 8)).astype(BF)
+            lhs.append(jnp.concatenate([value[a * 64 : (a + 1) * 64] for a in range(8)], axis=1))
+        packed = jnp.dot(jnp.concatenate(lhs, axis=0), pack[...], preferred_element_type=F32).astype(BF)
+        for row in range(4):
+            cs[row] = packed[row * 64 : (row + 1) * 64]
+        for d in range(1, 4):
+            coeff_copy(d).start()
+        cr[x] = cs[x]
+
+    def other_coefficients():
+        for d in range(1, 4):
+            coeff_copy(d).wait_recv()
+        lhs = jnp.concatenate([cr[a] for a in range(4)], axis=1)
+        wide = jnp.dot(lhs, unpack[...], preferred_element_type=F32).astype(BF)
+        return jnp.concatenate([wide[:, a * 128 : (a + 1) * 128] for a in range(8)], axis=0)
+
+    turn = (y % 4) * 2 + z // 4
 
     build_table(f, 0)
     loads[0].wait()
     dft(0)
-    pl.semaphore_wait(barrier, 24)
+    pl.semaphore_wait(barrier, 25)
     y_send(0)
+    mine[...] = jnp.full((8, 128), 1e9, F32)
+    mine[0:1, 0:40] = start_ref[1].astype(F32)
+    mine[0:1, 40:41] = jnp.max(start_ref[1] + rank_ref[1], axis=1, keepdims=True).astype(F32)
+    for d in range(1, 4):
+        meta_copy(d).start()
+    meta[x] = mine[...]
+    loads[1].wait()
+    for a in range(4):
+        v_copy(a, True).start()
+        v_copy((a + 2) % 4, False).start()
     build_table(f, 1)
     dft(1)
     y_send(1)
@@ -234,12 +310,20 @@
         )
     lane = lax.broadcasted_iota(jnp.int32, (512, 128), 1)
     slot40 = lax.broadcasted_iota(jnp.int32, (512, 40), 0)
-    for kk in range(2):
-        starts = start_ref[kk]
-        total = jnp.max(starts + rank_ref[kk], axis=1, keepdims=True)
-        begun = jnp.where(starts <= slot40, 1.0, 0.0) + jnp.where(total <= slot40, 64.0, 0.0)
-        owner = jnp.sum(begun, axis=1, keepdims=True).astype(jnp.int32) - 1
-        place[kk] = owner - 5 * (lane // 16)
+    starts = start_ref[0]
+    total = jnp.max(starts + rank_ref[0], axis=1, keepdims=True)
+    begun = jnp.where(starts <= slot40, 1.0, 0.0) + jnp.where(total <= slot40, 64.0, 0.0)
+    owner = jnp.sum(begun, axis=1, keepdims=True).astype(jnp.int32) - 1
+    place[...] = owner - 5 * (lane // 16)
+    row = lax.broadcasted_iota(jnp.int32, (1024, 128), 0)
+    col = lax.broadcasted_iota(jnp.int32, (1024, 128), 1)
+    pack[...] = jnp.where(col == (row // 128) * 16 + row % 16, 1.0, 0.0).astype(BF)
+    row = lax.broadcasted_iota(jnp.int32, (512, 128), 0)
+    col = lax.broadcasted_iota(jnp.int32, (512, 128), 1)
+    target = 64 + ((row // 8) % 2) * 32 + (row // 128) * 8 + (row % 8 + 8 - turn) % 8
+    for a in range(8):
+        hit = (col == target) & ((row // 16) % 8 == a)
+        unpack[:, pl.ds(a * 128, 128)] = jnp.where(hit, 1.0, 0.0).astype(BF)
     n = lax.broadcasted_iota(jnp.int32, (256, 256), 0)
     col = lax.broadcasted_iota(jnp.int32, (256, 256), 1)
     for c in range(2):
@@ -248,36 +332,37 @@
         for kk in range(2):
             table[kk * 2 + c] = jnp.dot(pick, f[kk], preferred_element_type=F32).astype(BF)
 
+    for d in range(1, 4):
+        meta_copy(d).wait_recv()
+    slot = lax.broadcasted_iota(jnp.int32, (512, 128), 0).astype(F32)
+    weight = jnp.where(lane == 40, 64.0, 1.0)
+    for row in range(4):
+        begun = jnp.where(meta[row, 0:1, :] <= slot, weight, 0.0)
+        owner = jnp.sum(begun, axis=1, keepdims=True).astype(jnp.int32) - 1
+        place4[row] = owner - 5 * (lane // 16)
+    for a in (0, 2, 1, 3):
+        v_pass(a)
     g_send(0)
     for i in range(8):
         forward(0, i)
-        if i >= 4:
-            relay(0, i - 4)
     g_send(1)
     for i in range(8, 16):
         forward(0, i)
-        relay(0, i - 4)
-    for i in range(4):
-        forward(1, i)
-        relay(0, 12 + i)
+    for i in range(16):
+        relay(0, i)
+    for a in range(4):
+        v_copy(a, a >= 2).wait_recv()
+    v_whole(vs.at[0], v2, None).wait_recv()
+    for i in range(15):
+        g_copy(1, i).wait_recv()
+    own_products()
+    for load in loads[2:]:
+        load.wait()
     settle(0)
-    for load in loads[1:]:
-        load.wait()
     for jj in range(5):
-        products(0, jj)
-        for i in range(4 + 2 * jj, 6 + 2 * jj):
-            forward(1, i)
-            relay(1, i - 4)
-    for i in range(14, 16):
-        forward(1, i)
-        relay(1, i - 4)
-    e = coefficients(0)
-    for i in range(12, 16):
-        relay(1, i)
-    settle(1)
-    for jj in range(5):
-        products(1, jj)
-    e = e + coefficients(1)
+        products(jj)
+    e = jnp.dot(u[0].reshape(512, 512), coefficients(), preferred_element_type=F32)
+    e = e + jnp.dot(u[1].reshape(512, 512), other_coefficients(), preferred_element_type=F32)
     bb[...] = (e[:256] + swapped(e[256:], 32)).astype(BF)
 
     def y_back(i):
@@ -317,9 +402,14 @@
             y_copy(kk, i).wait_send()
         for i in range(15):
             g_copy(kk, i).wait_send()
-        for a in range(2):
-            whole(kk, x, xs.at[kk, a], x2.at[kk]).wait_send()
-            whole(kk, x, xs2.at[kk, a], x2.at[kk], 640).wait_send()
+    for a in range(2):
+        whole(0, x, xs.at[0, a], x2.at[0]).wait_send()
+        whole(0, x, xs2.at[0, a], x2.at[0], 640).wait_send()
+        v_whole(vs.at[a], v2, None).wait_send()
+        v_whole(vs2.at[a], v2, 0).wait_send()
+    for d in range(1, 4):
+        meta_copy(d).wait_send()
+        coeff_copy(d).wait_send()
     for i in range(7):
         y_back(i).wait_send()
     for i in range(15):
@@ -339,17 +429,25 @@
         out_specs=VM,
         scratch_shapes=[
             pltpu.VMEM((640, 1024), BF),
-            pltpu.VMEM((2, 2, 512, 256), BF),
+            pltpu.VMEM((2, 512, 256), BF),
+            pltpu.VMEM((4, 2, 512, 256), BF),
             pltpu.VMEM((2, 2, 256, 512), BF),
             pltpu.VMEM((2, 256, 1024), BF),
             pltpu.VMEM((2, 640, 128), F32),
             pltpu.VMEM((2, 8, 80, 256), BF),
             pltpu.VMEM((2, 8, 80, 256), BF),
             pltpu.VMEM((1024, 1024), BF),
+            pltpu.VMEM((1024, 128), BF),
+            pltpu.VMEM((512, 1024), BF),
             pltpu.VMEM((2, 16, 80, 128), BF),
             pltpu.VMEM((4, 2, 1280, 128), BF),
-            pltpu.VMEM((2, 512, 128), jnp.int32),
+            pltpu.VMEM((8, 128), F32),
+            pltpu.VMEM((4, 8, 128), F32),
+            pltpu.VMEM((512, 128), jnp.int32),
+            pltpu.VMEM((4, 512, 128), jnp.int32),
             pltpu.VMEM((1024, 512), F32),
+            pltpu.VMEM((4, 64, 128), BF),
+            pltpu.VMEM((4, 64, 128), BF),
             pltpu.VMEM((4, 256, 1024), BF),
             pltpu.VMEM((256, 128), BF),
             pltpu.VMEM((8, 32, 128), BF),
@@ -369,6 +467,15 @@
             DMA((7,)),
             DMA((15,)),
             DMA((15,)),
+            DMA((2,)),
+            DMA((4,)),
+            DMA((4,)),
+            DMA,
+            DMA((2,)),
+            DMA((3,)),
+            DMA((3,)),
+            DMA((3,)),
+            DMA((3,)),
         ],
         compiler_params=pltpu.CompilerParams(
             collective_id=0, has_side_effects=True, vmem_limit_bytes=56 * 1024 * 1024

time: 80.1 us -> 67 us (0.84)
  Pallas kernels: 78.4 us -> 65.3 us
    pallas_call x1, Pallas kernels: 78.4 us -> 65.3 us  [per_device(): pl.pallas_call(kernel, out_shape=jax.ShapeDtypeStruct((64, 1024), BF), in...]
where the time goes in v3:
time: 67 us; the launch traced here: 66.8 us
  Pallas kernels  65.3 us (97%)
  local copies, waits for them, and re-layouts  1.57 us (2%)
    pallas_call x1, Pallas kernels, per_device(): pl.pallas_call(kernel, out_shape=jax.ShapeDtypeStruct((64, 1024), BF), in...  65.3 us
    unnamed x1, local copies, waits for them, and re-layouts  1.57 us

profile of v3, /device:TPU:1, one launch (start us, length us, event | category | flops | bytes accessed | tf_op | source)
XLA Modules:
  0.0 66.8 jit_solution(1797980333810677029)
XLA Ops:
  0.0 65.3 %shard_map.55 = bf16[64,1024]{1,0:T(8,128)(2,1)} custom-call(bf16[640,1024]{1,0:T(8,128)(2,1)} %bitcast.4, bf16[2,2,512,256]{3,2,1,0:T(8,128)(2,1)} %bitcast.5, bf16[2,2,256,512]{3,2,1,0:T(8,128)(2,1)} %bitcast.6, s32[2,1,40]{2,1,0:T(1,128)} %rank_ref.1, s32[2,1,40]{2,1,0:T(1,128)} %start_ref.1), custom_call_target="tpu_custom_call" | custom-call | tf_op jit(solution)/shard_map/pallas_call | solution.py:425
  65.3 1.6 %copy.7 = bf16[2,32,1024]{2,1,0:T(8,128)(2,1)} copy(bf16[2,32,1024]{2,1,0:T(8,128)(2,1)} %bitcast.7) | data formatting | bytes 262144

commit v4 on v3

--- a/solution.py
+++ b/solution.py
@@ -18,7 +18,7 @@
 _z = 0.125 * (1.0 - np.cos(np.pi * (np.arange(64) + 0.5) / 64))
 COS = [float(a) for a in np.polynomial.polynomial.polyfit(_z, np.cos(2 * np.pi * np.sqrt(_z)), 9)]
 
-STEPS = [(0, 1)] + [(d, c) for d in (1, 7, 4, 3, 5, 2, 6) for c in (0, 1)]
+STEPS = [(0, 1)] + [(d, c) for d in (1, 7, 4, 5, 3, 2, 6) for c in (0, 1)]
 YSTEPS = (4, 3, 5, 2, 6, 1, 7)
 
 
@@ -58,10 +58,10 @@
 
 
 def kernel(
-    w_hbm, v_hbm, u_hbm, rank_ref, start_ref, out_ref,
-    w, v, vg, u, f, o, s1, r1, perm, pack, unpack, p2, g, mine, meta, place, place4, acc, cs, cr,
+    w_hbm, v_hbm, u_hbm, rank_hbm, start_hbm, out_ref,
+    rank_ref, start_ref, w, v, vg, u, f, o, s1, r1, perm, pack, unpack, p2, g, mine, meta, place, place4, acc, cs, cr,
     table, bb, ry, pz, rz,
-    load_sem, s1s, r1s, p2s, p2r, xs, xm, xp, x2, xs2, f1s, f1r, f2s, f2r,
+    load_sem, s1s, r1s, p2s, p2r, xs, xm, xp, x2, xs2, fs,
     vs, vm, vp, v2, vs2, ms, mr, css, crs,
 ):
     y = lax.axis_index("freq_0")
@@ -76,6 +76,8 @@
         pltpu.make_async_copy(v_hbm.at[:, 0], v, load_sem.at[2]),
         pltpu.make_async_copy(u_hbm.at[:, 0], u.at[0], load_sem.at[3]),
         pltpu.make_async_copy(u_hbm.at[:, 1], u.at[1], load_sem.at[4]),
+        pltpu.make_async_copy(rank_hbm, rank_ref, load_sem.at[5]),
+        pltpu.make_async_copy(start_hbm, start_ref, load_sem.at[6]),
     ]
     for load in loads:
         load.start()
@@ -109,29 +111,36 @@
 
     def y_copy(kk, i):
         d = YSTEPS[i]
-        return send(s1.at[kk, (y + d) % 8], r1.at[kk, y], s1s.at[kk, i], r1s.at[kk, i], y_peer(d))
+        return send(s1.at[kk, (y + d) % 8], r1.at[kk, y], s1s.at[kk], r1s.at[kk], y_peer(d))
+
+    def y_all(kk):
+        ref = r1.at[kk, pl.ds(0, 7)]
+        return send(ref, ref, s1s.at[kk], r1s.at[kk], y_peer(1))
 
     def g_copy(kk, i):
         d = STEPS[i]
         rows = pl.ds(me_g * 80, 80)
-        return send(p2.at[kk, g_to(d)], g.at[x, kk, rows], p2s.at[kk, i], p2r.at[kk, i], g_peer(d))
-
-    def block(kk, i, owner):
-        gs = me_g if i == 0 else g_from(STEPS[i - 1])
-        return g.at[owner, kk, pl.ds(gs * 80, 80)]
-
-    def x_copy(kk, i, up):
-        ref = block(kk, i, x)
+        return send(p2.at[kk, g_to(d)], g.at[x, kk, rows], p2s.at[kk], p2r.at[15 if kk else i], g_peer(d))
+
+    def g_all(kk):
+        ref = g.at[x, kk, pl.ds(0, 1200)]
+        return send(ref, ref, p2s.at[kk], p2r.at[15], g_peer(STEPS[0]))
+
+    def block(gs, owner):
+        return g.at[owner, 0, pl.ds(gs * 80, 80)]
+
+    def x_copy(gs, up):
+        ref = block(gs, x)
         if up:
-            return send(ref, ref, xs.at[kk, 0], xm.at[kk, i], {"rows": x_up})
-        return send(ref, ref, xs.at[kk, 1], xp.at[kk, i], {"rows": x_down})
-
-    def x_relay(kk, i):
-        if i % 2 == 0:
-            ref = block(kk, i, x_down)
-            return send(ref, ref, xs2.at[kk, 0], x2.at[kk], {"rows": x_up})
-        ref = block(kk, i, x_up)
-        return send(ref, ref, xs2.at[kk, 1], x2.at[kk], {"rows": x_down})
+            return send(ref, ref, xs.at[0], xm.at[8 - (8 - gs // 2) * (1 - gs % 2)], {"rows": x_up})
+        return send(ref, ref, xs.at[1], xp.at[8 - (8 - gs // 2) * (gs % 2)], {"rows": x_down})
+
+    def x_relay(gs):
+        if gs % 2 == 0:
+            ref = block(gs, x_down)
+            return send(ref, ref, xs2.at[0], x2.at[gs // 4], {"rows": x_up})
+        ref = block(gs, x_up)
+        return send(ref, ref, xs2.at[1], x2.at[gs // 4], {"rows": x_down})
 
     def v_copy(a, up):
         ref = vg.at[x, a // 2, pl.ds((a % 2) * 256, 256)]
@@ -152,10 +161,14 @@
         v_relay(a).start()
 
     def meta_copy(d):
-        return send(mine, meta.at[x], ms.at[d - 1], mr.at[d - 1], {"rows": (x + d) % 4})
+        return send(mine, meta.at[x], ms, mr, {"rows": (x + d) % 4})
+
+    meta_all = send(meta.at[pl.ds(0, 3)], meta.at[pl.ds(0, 3)], ms, mr, {"rows": x_up})
 
     def coeff_copy(d):
-        return send(cs.at[(x + d) % 4], cr.at[x], css.at[d - 1], crs.at[d - 1], {"rows": (x + d) % 4})
+        return send(cs.at[(x + d) % 4], cr.at[x], css, crs, {"rows": (x + d) % 4})
+
+    coeffs_all = send(cs.at[pl.ds(0, 3)], cr.at[pl.ds(0, 3)], css, crs, {"rows": x_up})
 
     def v_whole(ssem, rsem, part):
         ref = vg.at[x] if part is None else vg.at[x, part]
@@ -190,8 +203,7 @@
         r1[kk, y] = s1[kk, y]
 
     def g_send(kk):
-        for i in range(7):
-            y_copy(kk, i).wait_recv()
+        y_all(kk).wait_recv()
         lhs = jnp.concatenate(
             [
                 jnp.concatenate([r1[kk, a, :, pl.ds(h * 128, 128)] for a in range(8)], axis=1)
@@ -199,32 +211,39 @@
             ],
             axis=0,
         )
-        for b in range(8):
-            moved = jnp.dot(lhs, perm[:, pl.ds(b * 128, 128)], preferred_element_type=F32).astype(BF)
-            p2[kk, b] = moved[:80]
-            p2[kk, 8 + b] = moved[80:]
-        for i in range(15):
-            g_copy(kk, i).start()
-        g[x, kk, pl.ds(pl.multiple_of(me_g * 80, 16), 80)] = p2[kk, me_g]
-
-    def forward(kk, i):
+        for dz in (0, 1, 3, 2):
+            b = ((z + dz) % 4) * 2
+            cols = pl.ds(pl.multiple_of(b * 128, 256), 256)
+            moved = jnp.dot(lhs, perm[:, cols], preferred_element_type=F32).astype(BF)
+            for c in range(2):
+                p2[kk, b + c] = moved[:80, c * 128 : (c + 1) * 128]
+                p2[kk, 8 + b + c] = moved[80:, c * 128 : (c + 1) * 128]
+            for d in (dz, dz + 4):
+                for dc in (1, 0):
+                    if (d, dc) == (0, 0):
+                        g[x, kk, pl.ds(pl.multiple_of(me_g * 80, 16), 80)] = p2[kk, me_g]
+                    else:
+                        g_copy(kk, STEPS.index((d, dc))).start()
+
+    def forward(i):
+        gs = me_g
         if i > 0:
-            g_copy(kk, i - 1).wait_recv()
-        x_copy(kk, i, True).start()
-        x_copy(kk, i, False).start()
-
-    def relay(kk, i):
-        x_copy(kk, i, i % 2 == 0).wait_recv()
-        x_relay(kk, i).start()
+            g_copy(0, i - 1).wait_recv()
+            gs = g_from(STEPS[i - 1])
+        x_copy(gs, True).start()
+        x_copy(gs, False).start()
+
+    def relay(gs):
+        x_copy(gs, gs % 2 == 0).wait_recv()
+        x_relay(gs).start()
 
     def whole(kk, owner, ssem, rsem, rows=1280):
         ref = g.at[owner, kk, pl.ds(0, rows)]
         return send(ref, ref, ssem, rsem, {"rows": x_up})
 
-    def settle(kk):
-        for i in range(16):
-            x_copy(kk, i, i % 2 == 1).wait_recv()
-        whole(kk, x, xs.at[kk, 0], x2.at[kk]).wait_recv()
+    def settle():
+        whole(0, x, xs.at[0], xm.at[8], 640).wait_recv()
+        whole(0, x, xs.at[0], xp.at[8], 640).wait_recv()
 
     def products(jj):
         for half in range(2):
@@ -252,32 +271,31 @@
         return total.astype(BF)
 
     def own_products():
-        lhs = []
-        for row in range(4):
+        pairs = ((0, 1), (2, 3), (4,))
+        for d in (2, 1, 3, 0):
+            row = (x + d) % 4
             factors = vg[row].reshape(1024, 256)
-            for pair in ((0, 1), (2, 3), (4,)):
+            lanes = pl.ds(d * 128, 128)
+            for pair in pairs:
                 rhs = jnp.concatenate([g[x, 1, pl.ds(jj * 256, 256), :] for jj in pair], axis=1)
                 prod = jnp.dot(factors, rhs, preferred_element_type=F32)
                 for m, jj in enumerate(pair):
                     hit = place4[row] == jj
                     for ab in range(2):
                         rows = pl.ds(ab * 512, 512)
-                        old = acc[rows, pl.ds(row * 128, 128)] if jj else 0.0
+                        old = acc[rows, lanes] if jj else 0.0
                         new = prod[ab * 512 : (ab + 1) * 512, m * 128 : (m + 1) * 128]
-                        acc[rows, pl.ds(row * 128, 128)] = jnp.where(hit, new, old)
-            lanes = pl.ds(row * 128, 128)
+                        acc[rows, lanes] = jnp.where(hit, new, old)
             value = (acc[pl.ds(0, 512), lanes] + swapped(acc[pl.ds(512, 512), lanes], 8)).astype(BF)
-            lhs.append(jnp.concatenate([value[a * 64 : (a + 1) * 64] for a in range(8)], axis=1))
-        packed = jnp.dot(jnp.concatenate(lhs, axis=0), pack[...], preferred_element_type=F32).astype(BF)
-        for row in range(4):
-            cs[row] = packed[row * 64 : (row + 1) * 64]
-        for d in range(1, 4):
-            coeff_copy(d).start()
-        cr[x] = cs[x]
+            wide = jnp.concatenate([value[a * 64 : (a + 1) * 64] for a in range(8)], axis=1)
+            cs[row] = jnp.dot(wide, pack[...], preferred_element_type=F32).astype(BF)
+            if d:
+                coeff_copy(d).start()
+            else:
+                cr[x] = cs[x]
 
     def other_coefficients():
-        for d in range(1, 4):
-            coeff_copy(d).wait_recv()
+        coeffs_all.wait_recv()
         lhs = jnp.concatenate([cr[a] for a in range(4)], axis=1)
         wide = jnp.dot(lhs, unpack[...], preferred_element_type=F32).astype(BF)
         return jnp.concatenate([wide[:, a * 128 : (a + 1) * 128] for a in range(8)], axis=0)
@@ -289,6 +307,8 @@
     dft(0)
     pl.semaphore_wait(barrier, 25)
     y_send(0)
+    loads[5].wait()
+    loads[6].wait()
     mine[...] = jnp.full((8, 128), 1e9, F32)
     mine[0:1, 0:40] = start_ref[1].astype(F32)
     mine[0:1, 40:41] = jnp.max(start_ref[1] + rank_ref[1], axis=1, keepdims=True).astype(F32)
@@ -332,8 +352,7 @@
         for kk in range(2):
             table[kk * 2 + c] = jnp.dot(pick, f[kk], preferred_element_type=F32).astype(BF)
 
-    for d in range(1, 4):
-        meta_copy(d).wait_recv()
+    meta_all.wait_recv()
     slot = lax.broadcasted_iota(jnp.int32, (512, 128), 0).astype(F32)
     weight = jnp.where(lane == 40, 64.0, 1.0)
     for row in range(4):
@@ -343,23 +362,24 @@
     for a in (0, 2, 1, 3):
         v_pass(a)
     g_send(0)
-    for i in range(8):
-        forward(0, i)
+    for i in range(3):
+        forward(i)
     g_send(1)
-    for i in range(8, 16):
-        forward(0, i)
+    for i in range(3, 16):
+        forward(i)
     for i in range(16):
-        relay(0, i)
+        relay(i)
     for a in range(4):
         v_copy(a, a >= 2).wait_recv()
     v_whole(vs.at[0], v2, None).wait_recv()
-    for i in range(15):
-        g_copy(1, i).wait_recv()
+    g_all(1).wait_recv()
     own_products()
-    for load in loads[2:]:
+    for load in loads[2:5]:
         load.wait()
-    settle(0)
+    settle()
     for jj in range(5):
+        if jj < 4:
+            whole(0, x, xs.at[0], x2.at[jj], 320).wait_recv()
         products(jj)
     e = jnp.dot(u[0].reshape(512, 512), coefficients(), preferred_element_type=F32)
     e = e + jnp.dot(u[1].reshape(512, 512), other_coefficients(), preferred_element_type=F32)
@@ -368,26 +388,27 @@
     def y_back(i):
         d = YSTEPS[i]
         rows = pl.ds(pl.multiple_of(((y + d) % 8) * 32, 32), 32)
-        return send(bb.at[rows], ry.at[y], f1s.at[i], f1r.at[i], y_peer(d))
+        return send(bb.at[rows], ry.at[y], fs.at[0], fs.at[1], y_peer(d))
 
     def g_back(i):
         d = STEPS[i]
-        return send(pz.at[g_to(d)], rz.at[me_g], f2s.at[i], f2r.at[i], g_peer(d))
+        return send(pz.at[g_to(d)], rz.at[me_g], fs.at[2], fs.at[3], g_peer(d))
+
+    y_back_all = send(ry.at[pl.ds(0, 7)], ry.at[pl.ds(0, 7)], fs.at[0], fs.at[1], y_peer(1))
+    g_back_all = send(rz.at[pl.ds(0, 15)], rz.at[pl.ds(0, 15)], fs.at[2], fs.at[3], g_peer(STEPS[0]))
 
     for i in range(7):
         y_back(i).start()
     ry[y] = bb[pl.ds(pl.multiple_of(y * 32, 32), 32)]
     source = (n % 8) * 32 + (n // 16) * 2 + (n // 8) % 2
     pick = jnp.where(col == source, 1.0, 0.0).astype(BF)
-    for i in range(7):
-        y_back(i).wait_recv()
+    y_back_all.wait_recv()
     moved = jnp.dot(pick, ry[...].reshape(256, 128), preferred_element_type=F32)
     pz[...] = moved.astype(BF).reshape(16, 16, 128)
     for i in range(15):
         g_back(i).start()
     rz[me_g] = pz[me_g]
-    for i in range(15):
-        g_back(i).wait_recv()
+    g_back_all.wait_recv()
     turned = jnp.transpose(rz[...].reshape(256, 128).astype(F32))
     lane = lax.broadcasted_iota(jnp.int32, (32, 256), 1)
     series = jnp.zeros((64, 1024), F32)
@@ -398,22 +419,17 @@
     out_ref[...] = series.astype(BF)
 
     for kk in range(2):
-        for i in range(7):
-            y_copy(kk, i).wait_send()
-        for i in range(15):
-            g_copy(kk, i).wait_send()
+        y_all(kk).wait_send()
+        g_all(kk).wait_send()
     for a in range(2):
-        whole(0, x, xs.at[0, a], x2.at[0]).wait_send()
-        whole(0, x, xs2.at[0, a], x2.at[0], 640).wait_send()
+        whole(0, x, xs.at[a], x2.at[0]).wait_send()
+        whole(0, x, xs2.at[a], x2.at[0], 640).wait_send()
         v_whole(vs.at[a], v2, None).wait_send()
         v_whole(vs2.at[a], v2, 0).wait_send()
-    for d in range(1, 4):
-        meta_copy(d).wait_send()
-        coeff_copy(d).wait_send()
-    for i in range(7):
-        y_back(i).wait_send()
-    for i in range(15):
-        g_back(i).wait_send()
+    meta_all.wait_send()
+    coeffs_all.wait_send()
+    y_back_all.wait_send()
+    g_back_all.wait_send()
 
 
 VM = pl.BlockSpec(memory_space=pltpu.VMEM)
@@ -424,10 +440,12 @@
 def per_device(wavefield, u_factors, v_factors, tile_ranks, tile_offsets):
     series = pl.pallas_call(
         kernel,
-        out_shape=jax.ShapeDtypeStruct((64, 1024), BF),
-        in_specs=[ANY, ANY, ANY, VM, VM],
+        out_shape=pltpu.VMEM((64, 1024), BF),
+        in_specs=[ANY] * 5,
         out_specs=VM,
         scratch_shapes=[
+            pltpu.VMEM((2, 1, 40), jnp.int32),
+            pltpu.VMEM((2, 1, 40), jnp.int32),
             pltpu.VMEM((640, 1024), BF),
             pltpu.VMEM((2, 512, 256), BF),
             pltpu.VMEM((4, 2, 512, 256), BF),
@@ -453,29 +471,26 @@
             pltpu.VMEM((8, 32, 128), BF),
             pltpu.VMEM((16, 16, 128), BF),
             pltpu.VMEM((16, 16, 128), BF),
-            DMA((5,)),
-            DMA((2, 7)),
-            DMA((2, 7)),
-            DMA((2, 15)),
-            DMA((2, 15)),
-            DMA((2, 2)),
-            DMA((2, 16)),
-            DMA((2, 16)),
-            DMA((2,)),
-            DMA((2, 2)),
             DMA((7,)),
-            DMA((7,)),
-            DMA((15,)),
-            DMA((15,)),
+            DMA((2,)),
+            DMA((2,)),
+            DMA((2,)),
+            DMA((16,)),
+            DMA((2,)),
+            DMA((9,)),
+            DMA((9,)),
+            DMA((4,)),
+            DMA((2,)),
+            DMA((4,)),
             DMA((2,)),
             DMA((4,)),
             DMA((4,)),
             DMA,
             DMA((2,)),
-            DMA((3,)),
-            DMA((3,)),
-            DMA((3,)),
-            DMA((3,)),
+            DMA,
+            DMA,
+            DMA,
+            DMA,
         ],
         compiler_params=pltpu.CompilerParams(
             collective_id=0, has_side_effects=True, vmem_limit_bytes=56 * 1024 * 1024

time: 67 us -> 61.8 us (0.922)
  Pallas kernels: 65.3 us -> 61 us
  local copies, waits for them, and re-layouts: 1.57 us -> 0.66 us
    pallas_call x1, Pallas kernels: 65.3 us -> 61 us  [per_device(): pl.pallas_call(kernel, out_shape=pltpu.VMEM((64, 1024), BF), in_specs=[AN...]
    unnamed x1, local copies, waits for them, and re-layouts: 1.57 us -> 0.66 us
where the time goes in v4:
time: 61.8 us; the launch traced here: 61.7 us
  Pallas kernels  61 us (99%)
  local copies, waits for them, and re-layouts  0.66 us (1%)
    pallas_call x1, Pallas kernels, per_device(): pl.pallas_call(kernel, out_shape=pltpu.VMEM((64, 1024), BF), in_specs=[AN...  61 us

profile of v4, /device:TPU:1, one launch (start us, length us, event | category | flops | bytes accessed | tf_op | source)
XLA Modules:
  0.0 61.7 jit_solution(17977726811889406501)
XLA Ops:
  0.0 61.0 %shard_map.55 = bf16[64,1024]{1,0:T(8,128)(2,1)S(1)} custom-call(bf16[640,1024]{1,0:T(8,128)(2,1)} %bitcast.5, bf16[2,2,512,256]{3,2,1,0:T(8,128)(2,1)} %bitcast.6, bf16[2,2,256,512]{3,2,1,0:T(8,128)(2,1)} %bitcast.7, s32[2,1,40]{2,1,0:T(1,128)} %rank_hbm.1, s32[2,1,40]{2,1,0:T(1,128)} %start_hbm.1), custom_call_target="tpu_custom_call" | custom-call | tf_op jit(solution)/shard_map/pallas_call | solution.py:441
  61.0 0.7 %copy.7 = bf16[2,32,1024]{2,1,0:T(8,128)(2,1)} copy(bf16[2,32,1024]{2,1,0:T(8,128)(2,1)S(1)} %bitcast.4) | data formatting | bytes 262144

commit v5 on v4

--- a/solution.py
+++ b/solution.py
@@ -32,14 +32,16 @@
 
 
 def build_table(f_ref, kk):
+    turn = (((lax.broadcasted_iota(jnp.int32, (8, 128), 0) // 2) * 2 + (kk + 1)) * 128) & 1023
+    cos8 = jnp.concatenate([cosine(turn)] * 8, axis=0)
+    sin8 = jnp.concatenate([cosine((turn + 768) & 1023)] * 8, axis=0)
     for part in range(4):
         row = lax.broadcasted_iota(jnp.int32, (64, 128), 0) + part * 64
         lane = lax.broadcasted_iota(jnp.int32, (64, 128), 1)
         k1 = (row // 2) * 2 + (kk + 1)
         m = (k1 * lane + (row % 2) * 256) & 1023
         co, si = cosine(m), cosine((m + 768) & 1023)
-        turn = (k1 * 128) & 1023
-        ct, st = cosine(turn), cosine((turn + 768) & 1023)
+        ct, st = cos8, sin8
         for b in range(8):
             f_ref[kk, pl.ds(part * 64, 64), pl.ds(b * 128, 128)] = (co * (1.0 / 32.0)).astype(BF)
             if b < 7:
@@ -79,9 +81,6 @@
         pltpu.make_async_copy(rank_hbm, rank_ref, load_sem.at[5]),
         pltpu.make_async_copy(start_hbm, start_ref, load_sem.at[6]),
     ]
-    for load in loads:
-        load.start()
-
     def y_peer(d):
         return {"freq_0": (y + d) % 8}
 
@@ -97,12 +96,15 @@
     x_up, x_down = (x + 1) % 4, (x + 3) % 4
 
     barrier = pltpu.get_barrier_semaphore()
+    loads[0].start()
+    for d in sorted(STEPS, key=lambda d: -min(d[0], 8 - d[0])):
+        pl.semaphore_signal(barrier, inc=1, device_id=g_peer(d), device_id_type=MESH)
     for d in YSTEPS:
         pl.semaphore_signal(barrier, inc=1, device_id=y_peer(d), device_id_type=MESH)
-    for d in STEPS:
-        pl.semaphore_signal(barrier, inc=1, device_id=g_peer(d), device_id_type=MESH)
-    for peer in (x_up, x_down, (x + 2) % 4):
+    for peer in ((x + 2) % 4, x_up, x_down):
         pl.semaphore_signal(barrier, inc=1, device_id={"rows": peer}, device_id_type=MESH)
+    for load in loads[1:]:
+        load.start()
 
     def send(src, dst, ssem, rsem, peer):
         return pltpu.make_async_remote_copy(
@@ -175,27 +177,26 @@
         return send(ref, ref, ssem, rsem, {"rows": x_up})
 
     def dft(kk):
+        both = lax.dot_general(w[...], f[kk], (((1,), (1,)), ((), ())), preferred_element_type=F32)
         for half in range(2):
-            o[half] = lax.dot_general(
-                w[...], f[kk, pl.ds(half * 128, 128)], (((1,), (1,)), ((), ())), preferred_element_type=F32
-            )
+            o[half] = both[:, half * 128 : (half + 1) * 128]
         slot = lax.broadcasted_iota(jnp.int32, (16, 128), 1) // 16
+        bits = [(slot // 2**a) % 2 == 1 for a in range(3)]
 
         def place_rows(chunk, carry):
             for half in range(2):
-                turned = []
+                value = [None] * 8
                 for s in range(8):
                     t = o[half, pl.ds(chunk * 128 + s, 16, stride=8), :]
-                    turned.append(pltpu.roll(t, 16 * s, axis=1) if s else t)
+                    value[(-s) % 8] = pltpu.roll(t, 16 * s, axis=1) if s else t
+                for a in range(3):
+                    value = [jnp.where(bits[a], value[(b - 2**a) % 8], value[b]) for b in range(8)]
                 for b in range(8):
-                    value = turned[(-b) % 8]
-                    for q in range(1, 8):
-                        value = jnp.where(slot == q, turned[(q - b) % 8], value)
                     rows = pl.ds(pl.multiple_of(chunk * 16, 16), 16)
-                    s1[kk, half * 4 + b // 2, rows, pl.ds((b % 2) * 128, 128)] = value.astype(BF)
+                    s1[kk, half * 4 + b // 2, rows, pl.ds((b % 2) * 128, 128)] = value[b].astype(BF)
             return carry
 
-        lax.fori_loop(0, 5, place_rows, 0)
+        lax.fori_loop(0, 5, place_rows, 0, unroll=True)
 
     def y_send(kk):
         for i in range(7):
@@ -245,50 +246,40 @@
         whole(0, x, xs.at[0], xm.at[8], 640).wait_recv()
         whole(0, x, xs.at[0], xp.at[8], 640).wait_recv()
 
-    def products(jj):
-        for half in range(2):
-            rows = pl.ds(jj * 256, 256)
-            rhs = jnp.concatenate([g[2 * half, 0, rows, :], g[2 * half + 1, 0, rows, :]], axis=1)
-            prod = jnp.dot(v[...].reshape(1024, 256), rhs, preferred_element_type=F32)
-            for m in range(2):
-                hit = place[...] == jj
-                lanes = pl.ds((2 * half + m) * 128, 128)
-                for ab in range(2):
-                    old = acc[pl.ds(ab * 512, 512), lanes] if jj else 0.0
-                    new = prod[ab * 512 : (ab + 1) * 512, m * 128 : (m + 1) * 128]
-                    acc[pl.ds(ab * 512, 512), lanes] = jnp.where(hit, new, old)
-
-    def coefficients():
+    def products(factors, tiles, kk, source, owner, lanes):
+        rhs = jnp.concatenate([g[source, kk, pl.ds(jj * 256, 256), :] for jj in tiles], axis=1)
+        prod = jnp.dot(factors, rhs, preferred_element_type=F32)
+        for m, jj in enumerate(tiles):
+            hit = owner == jj
+            for ab in range(2):
+                rows = pl.ds(ab * 512, 512)
+                old = acc[rows, lanes] if jj else 0.0
+                new = prod[ab * 512 : (ab + 1) * 512, m * 128 : (m + 1) * 128]
+                acc[rows, lanes] = jnp.where(hit, new, old)
+
+    def combined(lanes):
+        return (acc[pl.ds(0, 512), lanes] + swapped(acc[pl.ds(512, 512), lanes], 8)).astype(BF)
+
+    def half_coefficients(d):
         row = lax.broadcasted_iota(jnp.int32, (128, 128), 0)
         col = lax.broadcasted_iota(jnp.int32, (128, 128), 1)
         c, s = (row // 8) % 2, (row % 8 + 8 - turn) % 8
-        total = jnp.zeros((512, 128), F32)
-        for b in range(4):
-            lanes = pl.ds(b * 128, 128)
-            value = acc[pl.ds(0, 512), lanes] + swapped(acc[pl.ds(512, 512), lanes], 8)
-            join = jnp.where(col == c * 32 + b * 8 + s, 1.0, 0.0).astype(BF)
-            total = total + jnp.dot(value.astype(BF), join, preferred_element_type=F32)
-        return total.astype(BF)
-
-    def own_products():
-        pairs = ((0, 1), (2, 3), (4,))
-        for d in (2, 1, 3, 0):
+        join = jnp.where(col == c * 32 + ((x + d) % 4) * 8 + s, 1.0, 0.0).astype(BF)
+        return jnp.dot(combined(pl.ds(d * 128, 128)), join, preferred_element_type=F32)
+
+    def own_products(steps):
+        lhs = []
+        for d in steps:
             row = (x + d) % 4
             factors = vg[row].reshape(1024, 256)
             lanes = pl.ds(d * 128, 128)
-            for pair in pairs:
-                rhs = jnp.concatenate([g[x, 1, pl.ds(jj * 256, 256), :] for jj in pair], axis=1)
-                prod = jnp.dot(factors, rhs, preferred_element_type=F32)
-                for m, jj in enumerate(pair):
-                    hit = place4[row] == jj
-                    for ab in range(2):
-                        rows = pl.ds(ab * 512, 512)
-                        old = acc[rows, lanes] if jj else 0.0
-                        new = prod[ab * 512 : (ab + 1) * 512, m * 128 : (m + 1) * 128]
-                        acc[rows, lanes] = jnp.where(hit, new, old)
-            value = (acc[pl.ds(0, 512), lanes] + swapped(acc[pl.ds(512, 512), lanes], 8)).astype(BF)
-            wide = jnp.concatenate([value[a * 64 : (a + 1) * 64] for a in range(8)], axis=1)
-            cs[row] = jnp.dot(wide, pack[...], preferred_element_type=F32).astype(BF)
+            for tiles in ((0, 1), (2, 3), (4,)):
+                products(factors, tiles, 1, x, place4[row], lanes)
+            value = combined(lanes)
+            lhs.append(jnp.concatenate([value[a * 64 : (a + 1) * 64] for a in range(8)], axis=1))
+        packed = jnp.dot(jnp.concatenate(lhs, axis=0), pack[...], preferred_element_type=F32).astype(BF)
+        for m, d in enumerate(steps):
+            cs[(x + d) % 4] = packed[m * 64 : (m + 1) * 64]
             if d:
                 coeff_copy(d).start()
             else:
@@ -346,9 +337,11 @@
         unpack[:, pl.ds(a * 128, 128)] = jnp.where(hit, 1.0, 0.0).astype(BF)
     n = lax.broadcasted_iota(jnp.int32, (256, 256), 0)
     col = lax.broadcasted_iota(jnp.int32, (256, 256), 1)
+    n2 = lax.broadcasted_iota(jnp.int32, (128, 256), 0)
+    col2 = lax.broadcasted_iota(jnp.int32, (128, 256), 1)
     for c in range(2):
-        source = ((n % 8) * 16 + n // 16) * 2 + c
-        pick = jnp.where(col == source, 2.0, 0.0).astype(BF)
+        source = ((n2 % 8) * 16 + n2 // 8) * 2 + c
+        pick = jnp.where(col2 == source, 2.0, 0.0).astype(BF)
         for kk in range(2):
             table[kk * 2 + c] = jnp.dot(pick, f[kk], preferred_element_type=F32).astype(BF)
 
@@ -367,22 +360,33 @@
     g_send(1)
     for i in range(3, 16):
         forward(i)
-    for i in range(16):
+    for i in range(12):
         relay(i)
     for a in range(4):
         v_copy(a, a >= 2).wait_recv()
     v_whole(vs.at[0], v2, None).wait_recv()
     g_all(1).wait_recv()
-    own_products()
+    own_products((2, 1))
+    for i in range(12, 16):
+        relay(i)
+    own_products((3, 0))
     for load in loads[2:5]:
         load.wait()
     settle()
-    for jj in range(5):
-        if jj < 4:
-            whole(0, x, xs.at[0], x2.at[jj], 320).wait_recv()
-        products(jj)
-    e = jnp.dot(u[0].reshape(512, 512), coefficients(), preferred_element_type=F32)
-    e = e + jnp.dot(u[1].reshape(512, 512), other_coefficients(), preferred_element_type=F32)
+    factors = v[...].reshape(1024, 256)
+    total = jnp.zeros((512, 128), F32)
+    for d in (0, 1, 3):
+        for tiles in ((0, 1), (2, 3), (4,)):
+            products(factors, tiles, 0, (x + d) % 4, place[...], pl.ds(d * 128, 128))
+        total = total + half_coefficients(d)
+    for groups, tiles in (((0, 1), (0, 1)), ((2,), (2,)), ((3,), (3, 4))):
+        if tiles == (3, 4):
+            e = jnp.dot(u[1].reshape(512, 512), other_coefficients(), preferred_element_type=F32)
+        for a in groups:
+            whole(0, x, xs.at[0], x2.at[a], 320).wait_recv()
+        products(factors, tiles, 0, (x + 2) % 4, place[...], pl.ds(256, 128))
+    total = total + half_coefficients(2)
+    e = e + jnp.dot(u[0].reshape(512, 512), total.astype(BF), preferred_element_type=F32)
     bb[...] = (e[:256] + swapped(e[256:], 32)).astype(BF)
 
     def y_back(i):
@@ -409,12 +413,11 @@
         g_back(i).start()
     rz[me_g] = pz[me_g]
     g_back_all.wait_recv()
-    turned = jnp.transpose(rz[...].reshape(256, 128).astype(F32))
-    lane = lax.broadcasted_iota(jnp.int32, (32, 256), 1)
+    landed = rz[...].astype(F32)
+    turned = [jnp.transpose(landed[:, q * 8 : (q + 1) * 8].reshape(128, 128)) for q in range(2)]
     series = jnp.zeros((64, 1024), F32)
     for b in range(4):
-        part = turned[b * 32 : (b + 1) * 32]
-        lhs = jnp.concatenate([jnp.where((lane // 8) % 2 == q, part, 0.0) for q in range(2)], axis=0)
+        lhs = jnp.concatenate([turned[q][b * 32 : (b + 1) * 32] for q in range(2)], axis=0)
         series = series + jnp.dot(lhs.astype(BF), table[b], preferred_element_type=F32)
     out_ref[...] = series.astype(BF)
 
@@ -466,7 +469,7 @@
             pltpu.VMEM((1024, 512), F32),
             pltpu.VMEM((4, 64, 128), BF),
             pltpu.VMEM((4, 64, 128), BF),
-            pltpu.VMEM((4, 256, 1024), BF),
+            pltpu.VMEM((4, 128, 1024), BF),
             pltpu.VMEM((256, 128), BF),
             pltpu.VMEM((8, 32, 128), BF),
             pltpu.VMEM((16, 16, 128), BF),

time: 61.8 us -> 60.2 us (0.974)
  Pallas kernels: 61 us -> 59.4 us
    pallas_call x1, Pallas kernels: 61 us -> 59.4 us  [per_device(): pl.pallas_call(kernel, out_shape=pltpu.VMEM((64, 1024), BF), in_specs=[AN...]
where the time goes in v5:
time: 60.2 us; the launch traced here: 60.1 us
  Pallas kernels  59.4 us (99%)
  local copies, waits for them, and re-layouts  0.66 us (1%)
    pallas_call x1, Pallas kernels, per_device(): pl.pallas_call(kernel, out_shape=pltpu.VMEM((64, 1024), BF), in_specs=[AN...  59.4 us

profile of v5, /device:TPU:1, one launch (start us, length us, event | category | flops | bytes accessed | tf_op | source)
XLA Modules:
  0.0 60.1 jit_solution(4748667095170973798)
XLA Ops:
  0.0 59.4 %shard_map.55 = bf16[64,1024]{1,0:T(8,128)(2,1)S(1)} custom-call(bf16[640,1024]{1,0:T(8,128)(2,1)} %bitcast.5, bf16[2,2,512,256]{3,2,1,0:T(8,128)(2,1)} %bitcast.6, bf16[2,2,256,512]{3,2,1,0:T(8,128)(2,1)} %bitcast.7, s32[2,1,40]{2,1,0:T(1,128)} %rank_hbm.1, s32[2,1,40]{2,1,0:T(1,128)} %start_hbm.1), custom_call_target="tpu_custom_call" | custom-call | tf_op jit(solution)/shard_map/pallas_call | solution.py:444
  59.4 0.7 %copy.7 = bf16[2,32,1024]{2,1,0:T(8,128)(2,1)} copy(bf16[2,32,1024]{2,1,0:T(8,128)(2,1)S(1)} %bitcast.4) | data formatting | bytes 262144

commit v6 on v5

--- a/solution.py
+++ b/solution.py
@@ -360,33 +360,36 @@
     g_send(1)
     for i in range(3, 16):
         forward(i)
-    for i in range(12):
+    for load in loads[2:5]:
+        load.wait()
+    factors = v[...].reshape(1024, 256)
+
+    def source_block(d):
+        for tiles in ((0, 1), (2, 3), (4,)):
+            products(factors, tiles, 0, (x + d) % 4, place[...], pl.ds(d * 128, 128))
+        return half_coefficients(d)
+
+    total = source_block(0)
+    for i in range(14):
         relay(i)
     for a in range(4):
         v_copy(a, a >= 2).wait_recv()
     v_whole(vs.at[0], v2, None).wait_recv()
     g_all(1).wait_recv()
     own_products((2, 1))
-    for i in range(12, 16):
+    for i in range(14, 16):
         relay(i)
     own_products((3, 0))
-    for load in loads[2:5]:
-        load.wait()
     settle()
-    factors = v[...].reshape(1024, 256)
-    total = jnp.zeros((512, 128), F32)
-    for d in (0, 1, 3):
-        for tiles in ((0, 1), (2, 3), (4,)):
-            products(factors, tiles, 0, (x + d) % 4, place[...], pl.ds(d * 128, 128))
-        total = total + half_coefficients(d)
+    for d in (1, 3):
+        total = total + source_block(d)
     for groups, tiles in (((0, 1), (0, 1)), ((2,), (2,)), ((3,), (3, 4))):
-        if tiles == (3, 4):
-            e = jnp.dot(u[1].reshape(512, 512), other_coefficients(), preferred_element_type=F32)
         for a in groups:
             whole(0, x, xs.at[0], x2.at[a], 320).wait_recv()
         products(factors, tiles, 0, (x + 2) % 4, place[...], pl.ds(256, 128))
     total = total + half_coefficients(2)
-    e = e + jnp.dot(u[0].reshape(512, 512), total.astype(BF), preferred_element_type=F32)
+    e = jnp.dot(u[0].reshape(512, 512), total.astype(BF), preferred_element_type=F32)
+    e = e + jnp.dot(u[1].reshape(512, 512), other_coefficients(), preferred_element_type=F32)
     bb[...] = (e[:256] + swapped(e[256:], 32)).astype(BF)
 
     def y_back(i):
@@ -409,7 +412,7 @@
     y_back_all.wait_recv()
     moved = jnp.dot(pick, ry[...].reshape(256, 128), preferred_element_type=F32)
     pz[...] = moved.astype(BF).reshape(16, 16, 128)
-    for i in range(15):
+    for i in sorted(range(15), key=lambda i: -min(STEPS[i][0], 8 - STEPS[i][0])):
         g_back(i).start()
     rz[me_g] = pz[me_g]
     g_back_all.wait_recv()

time: 60.2 us -> 60 us (level)
  no operation moved by 1% of the time
where the time goes in v6:
time: 60 us; the launch traced here: 59.9 us
  Pallas kernels  59.2 us (99%)
  local copies, waits for them, and re-layouts  0.66 us (1%)
    pallas_call x1, Pallas kernels, per_device(): pl.pallas_call(kernel, out_shape=pltpu.VMEM((64, 1024), BF), in_specs=[AN...  59.2 us

profile of v6, /device:TPU:1, one launch (start us, length us, event | category | flops | bytes accessed | tf_op | source)
XLA Modules:
  0.0 59.9 jit_solution(1157365490050007211)
XLA Ops:
  0.0 59.2 %shard_map.55 = bf16[64,1024]{1,0:T(8,128)(2,1)S(1)} custom-call(bf16[640,1024]{1,0:T(8,128)(2,1)} %bitcast.5, bf16[2,2,512,256]{3,2,1,0:T(8,128)(2,1)} %bitcast.6, bf16[2,2,256,512]{3,2,1,0:T(8,128)(2,1)} %bitcast.7, s32[2,1,40]{2,1,0:T(1,128)} %rank_hbm.1, s32[2,1,40]{2,1,0:T(1,128)} %start_hbm.1), custom_call_target="tpu_custom_call" | custom-call | tf_op jit(solution)/shard_map/pallas_call | solution.py:447
  59.2 0.7 %copy.7 = bf16[2,32,1024]{2,1,0:T(8,128)(2,1)} copy(bf16[2,32,1024]{2,1,0:T(8,128)(2,1)S(1)} %bitcast.4) | data formatting | bytes 262144
